TPU v7x, 32 devices: a whole 2x2x4 slice. The times are simulated.
32 devices in a mesh: rep: 8 (over y, x, core), shard: 4 (over z).
Axes of the slice: x: 2, y: 2, z: 4, core: 2. Of those that a mesh axis runs over, the one named last changes fastest.
Arguments:
- activations: bfloat16 [6, 4096, 2048], P(None, ('rep', 'shard')), may hold values from -50 to 50
- cotangents: bfloat16 [6, 4096, 512], P(None, ('rep', 'shard')), may hold values from -120 to 120
- momentum: float32 [12, 256, 2048], P(None, None, 'shard'), may hold values from -6 to 6
- owners: int32 [12], replicated, may hold values from 0 to 3, as said below
- bucket_starts: int32 [2], replicated, may hold values from 1 to 11, as said below
Outputs:
- momentum_out: float32 [12, 256, 2048], P(None, None, 'shard')
- update: float32 [12, 256, 2048], P(None, None, 'shard')
- owned: bfloat16 [16, 256, 2048], P('shard')
Inputs may be any that keep to these rules, and one draw needn't show every extreme that they name: `owners`: no owner is named more than 4 times, and some owner exactly 4 times. `bucket_starts`: strictly increasing.
All inputs are finite; a program needn't handle non-finite values.
Results may differ from a plain program's by a relative error of at most 0.033.
Values may be sent and summed in bfloat16 or wider, within the bound.
A program may use at most 128 MiB of HBM per device.

v0:
```python
import functools
import math

import jax
import jax.numpy as jnp
from jax import lax
from jax.experimental import pallas as pl
from jax.experimental.pallas import tpu as pltpu
from jax.sharding import PartitionSpec as P

D = 2048
KV = 256
ITERS = 5
MATS = 12
MESH = pl.DeviceIdType.MESH
VMEM_SPEC = pl.BlockSpec(memory_space=pltpu.VMEM)
SMEM_SPEC = pl.BlockSpec(memory_space=pltpu.SMEM)
ANY_SPEC = pl.BlockSpec(memory_space=pl.ANY)
VMEM_LIMIT = 60 * 1024 * 1024

coef_a = 3.4445
coef_b = -4.775
coef_c = 2.0315
momentum_rate = 0.95
clip_level = 0.5
epsilon = 1e-06


def orthogonal_batch(matrices):
    values = matrices.astype(jnp.float32)
    frobenius = jnp.sqrt(jnp.sum(values * values, axis=(1, 2), keepdims=True))
    matrix = (values / (frobenius + epsilon)).astype(jnp.bfloat16)
    for iteration in range(ITERS):
        gram_matrix = jnp.einsum(
            "skd,sjd->skj", matrix, matrix, preferred_element_type=jnp.float32
        ).astype(jnp.bfloat16)
        square = jnp.einsum(
            "skj,sji->ski", gram_matrix, gram_matrix, preferred_element_type=jnp.float32
        )
        mixing = (coef_b * gram_matrix.astype(jnp.float32) + coef_c * square).astype(jnp.bfloat16)
        product = jnp.einsum("skj,sjd->skd", mixing, matrix, preferred_element_type=jnp.float32)
        matrix = (coef_a * matrix.astype(jnp.float32) + product).astype(jnp.bfloat16)
    return matrix


def clip_factors(square_sums, bucket_starts):
    indices = jnp.arange(MATS, dtype=jnp.int32)
    buckets = jnp.sum((indices[:, None] >= bucket_starts[None, :]).astype(jnp.int32), axis=1)
    together = (buckets[:, None] == buckets[None, :]).astype(jnp.float32)
    totals = jnp.sum(together * square_sums[None, :], axis=1)
    members = jnp.sum(together, axis=1)
    root_mean = jnp.sqrt(totals / (members * KV * D) + epsilon)
    return jnp.minimum(1.0, clip_level / root_mean)


def slot_numbers(owners):
    indices = jnp.arange(MATS, dtype=jnp.int32)
    earlier = (indices[None, :] < indices[:, None]) & (owners[None, :] == owners[:, None])
    return jnp.sum(earlier.astype(jnp.int32), axis=1)


def selector(owner_of, slot_of, shard_count, slot_count):
    holders = lax.broadcasted_iota(jnp.int32, (shard_count, slot_count, 1), 0)
    places = lax.broadcasted_iota(jnp.int32, (shard_count, slot_count, 1), 1)
    chosen = (holders == owner_of[None, None, :]) & (places == slot_of[None, None, :])
    return chosen.astype(jnp.bfloat16)


def pack_slots(shards, chooser):
    return jnp.einsum("psm,mkd->skpd", chooser, shards, preferred_element_type=jnp.float32).astype(
        jnp.bfloat16
    )


def unpack_slots(received, chooser):
    return jnp.einsum("psm,skpd->mkd", chooser, received, preferred_element_type=jnp.float32)


def per_device_general(activations, cotangents, momentum, owners, bucket_starts):
    shard_count = lax.axis_size("shard")
    replica_count = lax.axis_size("rep")
    layers, tok_rows, width = activations.shape
    token_total = tok_rows * shard_count * replica_count
    columns = width // shard_count
    slot_count = -(-MATS // shard_count) + 1
    update_scale = math.sqrt(max(KV, D))
    partial_terms = jnp.einsum(
        "ltk,ltd->lkd", cotangents, activations, preferred_element_type=jnp.float32
    ).reshape(MATS, KV, width)
    shard_part = lax.psum_scatter(
        partial_terms.astype(jnp.bfloat16), "shard", scatter_dimension=2, tiled=True
    )
    summed = lax.psum(shard_part, "rep").astype(jnp.float32)
    gradient = summed / jnp.sqrt(jnp.float32(token_total))
    square_sums = lax.psum(jnp.sum(gradient * gradient, axis=(1, 2)), "shard")
    factors = clip_factors(square_sums, bucket_starts)
    momentum_out = momentum_rate * momentum + factors[:, None, None] * gradient
    nesterov = (factors[:, None, None] * gradient + momentum_rate * momentum_out).astype(
        jnp.bfloat16
    )
    slot_of = slot_numbers(owners)
    chooser = selector(owners, slot_of, shard_count, slot_count)
    received = lax.all_to_all(
        pack_slots(nesterov, chooser), "shard", split_axis=2, concat_axis=2, tiled=True
    )
    item_count = received.shape[0]
    result = orthogonal_batch(received.reshape(item_count, KV, width))
    scaled = (update_scale * result.astype(jnp.float32)).astype(jnp.bfloat16)
    returned_part = lax.all_to_all(
        result.reshape(item_count, KV, shard_count, columns),
        "shard",
        split_axis=2,
        concat_axis=2,
        tiled=True,
    )
    update = update_scale * unpack_slots(returned_part, chooser)
    return (momentum_out, update, scaled)


def place():
    me = lax.axis_index("rep")
    core = lax.rem(me, 2)
    x = lax.rem(lax.div(me, 2), 2)
    y = lax.div(me, 4)
    to_core = me + 1 - 2 * core
    to_x = me + 2 - 4 * x
    to_y = me + 4 - 8 * y
    to_xy = me + 6 - 4 * x - 8 * y
    return me, core, x, y, to_core, to_x, to_y, to_xy


def greet(peers):
    barrier = pltpu.get_barrier_semaphore()
    for peer in peers:
        pl.semaphore_signal(barrier, inc=1, device_id=peer, device_id_type=MESH)
    pl.semaphore_wait(barrier, len(peers))


def remote(src, dst, send, recv, peer):
    return pltpu.make_async_remote_copy(
        src_ref=src, dst_ref=dst, send_sem=send, recv_sem=recv, device_id=peer, device_id_type=MESH
    )


def plane_gather_start(z, at, send, recv):
    me, core, x, y, to_core, to_x, to_y, to_xy = place()
    plan = ((0, to_x, 0), (2, to_y, 1), (1, to_x, 1), (3, to_y, 0), (4, to_core, None))
    copies = {}
    for k, peer, half in plan:
        copies[k] = remote(at(me, half), at(me, half), send.at[k], recv.at[k], (peer, z))
        copies[k].start()
    return copies


def plane_gather_turn(z, at, send, recv, copies):
    me, core, x, y, to_core, to_x, to_y, to_xy = place()

    def forward(k, block, half, peer):
        copies[k] = remote(
            at(block, half), at(block, half), send.at[k], recv.at[k], (peer, z)
        )
        copies[k].start()

    copies[0].wait_recv()
    forward(5, to_x, 0, to_y)
    copies[2].wait_recv()
    forward(6, to_y, 1, to_x)
    copies[1].wait_recv()
    forward(7, to_x, None, to_core)
    copies[3].wait_recv()
    forward(8, to_y, None, to_core)


def plane_gather_finish(z, at, send, recv, copies):
    me, core, x, y, to_core, to_x, to_y, to_xy = place()
    copies[5].wait_recv()
    copies[6].wait_recv()
    copies[9] = remote(
        at(to_xy, None), at(to_xy, None), send.at[9], recv.at[9], (to_core, z)
    )
    copies[9].start()
    for k in (4, 7, 8, 9):
        copies[k].wait_recv()
    for k in range(10):
        copies[k].wait_send()


def block_at(ref, axis):
    rows = ref.shape[axis] // 2

    def at(r, half):
        if half is None:
            return ref.at[r]
        cut = pl.ds(half * rows, rows)
        return ref.at[r, cut] if axis == 1 else ref.at[r, :, cut]

    return at


def plan_kernel(
    n_shard, groups, owner_of, lay_ref, half_ref, position_ref, block_ref, member_ref,
    mat_ref, place_ref, owner_ref, slot_ref, keep_ref, perm, sort,
):
    z = lax.axis_index("shard")
    group = lax.div(lax.axis_index("rep"), 2)
    members = owner_ref.shape[0]
    owners = [owner_of[m] for m in range(MATS)]
    one = lambda yes: yes.astype(jnp.int32)
    for m in range(MATS):
        rank = jnp.int32(0)
        for j in range(MATS):
            if j != m:
                rank += one(owners[j] <= owners[m] if j < m else owners[j] < owners[m])
        member = lax.div(rank, groups)
        block = lax.rem(rank, groups)
        position = block * members + member
        position_ref[m] = position
        block_ref[m] = 2 * block
        member_ref[m] = member
        lay_ref[position] = jnp.int32(m // 2)
        half_ref[position] = jnp.int32(m % 2)
        perm[position] = jnp.int32(m)
        sort[position] = owners[m]
    for j in range(members):
        owner_ref[j] = sort[group * members + j]
    for p in range(n_shard):
        first = jnp.int32(0)
        for m in range(MATS):
            first += one(owners[m] < p)
        skip = lax.rem(group + groups * MATS - first, groups)
        place = lax.div(jnp.minimum(first + skip, MATS - 1), groups)
        place_ref[p] = place
        mat_ref[p] = perm[group * members + place]
    start = jnp.int32(0)
    count = jnp.int32(0)
    for m in range(MATS):
        start += one(owners[m] < z)
        count += one(owners[m] == z)
    for i in range(slot_ref.shape[0]):
        slot_ref[i] = 2 * lax.rem(start + i, groups)
        keep_ref[i] = one(count > i)


def reduce_kernel(
    n_shard, inverse, lay_ref, half_ref, act_ref, cot_ref, gown_ref, sq_ref,
    act, cot, part, recv1, turn, recv2, plane, zrecv,
    local_sem, in_send, in_recv, s1, r1, s2, r2, s3, r3, gs, gr, qs, qr,
):
    me, core, x, y, to_core, to_x, to_y, to_xy = place()
    z = lax.axis_index("shard")
    tokens = act_ref.shape[1]
    rows, cols = part.shape[-2:]
    members = part.shape[2 + 1]
    steps = [d for d in (2, 1, 3) if d < n_shard] + list(range(4, n_shard)) + [0]
    other = 1 - 2 * core
    near = (to_core, to_x, to_y, to_xy, to_x + other, to_y + other, to_xy + other)
    peers = [(p, z) for p in near]
    peers += [(me, lax.rem(z + d, n_shard)) for d in range(1, n_shard)]
    cut = [
        pl.ds(pl.multiple_of(lax.rem(z + d, n_shard) * cols, cols), cols) for d in steps
    ]
    own = [
        pltpu.make_async_copy(
            act_ref.at[:, :, cut[k]], act[k].at[:, pl.ds(0, tokens)], local_sem.at[k]
        )
        for k in range(n_shard)
    ]
    own.append(
        pltpu.make_async_copy(cot_ref, cot.at[:, pl.ds(0, tokens)], local_sem.at[n_shard])
    )
    for c in own:
        c.start()
    greet(peers)
    theirs = pl.ds(tokens, tokens)
    swap = [
        remote(
            act_ref.at[:, :, cut[k]], act[k].at[:, theirs],
            in_send.at[k], in_recv.at[k], (to_core, z),
        )
        for k in range(n_shard)
    ]
    swap.append(
        remote(cot_ref, cot.at[:, theirs], in_send.at[n_shard], in_recv.at[n_shard], (to_core, z))
    )
    for c in swap[-1:] + swap[:-1]:
        c.start()
    for c in own:
        c.wait()
    swap[n_shard].wait()
    first = []
    second = []
    third = []

    def launch(k):
        swap[k].wait()

        def one(q, carry):
            group = lax.div(q, members)
            member = lax.rem(q, members)
            block = cot[lay_ref[q]]
            low = jnp.where(core == 0, block[:, :rows], block[:, rows : 2 * rows])
            high = jnp.where(core == 0, block[:, 2 * rows : 3 * rows], block[:, 3 * rows :])
            left = jnp.where(half_ref[q] == 0, low, high)
            right = act[k][lay_ref[q]]
            value = lax.dot_general(
                left, right, (((0,), (0,)), ((), ())), preferred_element_type=jnp.float32
            )
            part[k, lax.div(group, 2), lax.rem(group, 2), member] = value.astype(part.dtype)
            return carry

        lax.fori_loop(0, 4 * members, one, 0)

    def send_first(k):
        if k % 2 == 0:
            c = remote(part.at[k, :, 1 - x], recv1.at[k], s1.at[k], r1.at[k], (to_x, z))
        else:
            c = remote(part.at[k, 1 - y], recv1.at[k], s1.at[k], r1.at[k], (to_y, z))
        c.start()
        first.append(c)

    def send_second(k):
        first[k].wait_recv()

        def add_out(j, carry):
            if k % 2 == 0:
                mine = part[k, 1 - y, x, j]
                came = recv1[k, 1 - y, j]
            else:
                mine = part[k, y, 1 - x, j]
                came = recv1[k, 1 - x, j]
            turn[k, j] = (mine.astype(jnp.float32) + came.astype(jnp.float32)).astype(turn.dtype)
            return carry

        lax.fori_loop(0, members, add_out, 0)
        c = remote(
            turn.at[k], recv2.at[k], s2.at[k], r2.at[k], (to_y if k % 2 == 0 else to_x, z)
        )
        c.start()
        second.append(c)

    def send_third(k):
        second[k].wait_recv()

        def add_in(j, carry):
            came = recv1[k, y, j] if k % 2 == 0 else recv1[k, x, j]
            value = part[k, y, x, j].astype(jnp.float32) + came.astype(jnp.float32)
            value = value + recv2[k, j].astype(jnp.float32)
            plane[k, j] = value.astype(plane.dtype)
            return carry

        lax.fori_loop(0, members, add_in, 0)
        if steps[k]:
            c = remote(
                plane.at[k], zrecv.at[k], s3.at[k], r3.at[k],
                (me, lax.rem(z + steps[k], n_shard)),
            )
            c.start()
            third.append(c)

    launch(0)
    send_first(0)
    launch(1)
    send_first(1)
    for k in range(2, n_shard):
        launch(k)
    for k in range(0, n_shard, 2):
        pair = [i for i in (k, k + 1) if i < n_shard]
        for i in pair:
            send_second(i)
        for i in (k + 2, k + 3):
            if i < n_shard:
                send_first(i)
        for i in pair:
            send_third(i)
    for c in third:
        c.wait_recv()

    def add_last(j, carry):
        value = plane[n_shard - 1, j].astype(jnp.float32)
        for k in range(n_shard - 1):
            value = value + zrecv[k, j].astype(jnp.float32)
        value = (value * inverse).astype(gown_ref.dtype)
        gown_ref[core, j] = value
        value = value.astype(jnp.float32)
        line = jnp.sum(value * value, axis=0, keepdims=True)
        lanes = sq_ref.shape[-1]
        fold = line[:, :lanes]
        for i in range(1, cols // lanes):
            fold = fold + line[:, i * lanes : (i + 1) * lanes]
        sq_ref[0, me, j] = fold
        return carry

    lax.fori_loop(0, members, add_last, 0)
    fourth = []
    for k, peer in enumerate(near):
        c = remote(sq_ref.at[0, me], sq_ref.at[0, me], gs.at[k], gr.at[k], (peer, z))
        c.start()
        fourth.append(c)
    c = remote(gown_ref.at[core], gown_ref.at[core], gs.at[len(near)], gr.at[len(near)], (to_core, z))
    c.start()
    for f in fourth:
        f.wait_recv()
    for d in range(1, n_shard):
        f = remote(
            sq_ref.at[0], sq_ref.at[d], qs.at[d - 1], qr.at[d - 1],
            (me, lax.rem(z + d, n_shard)),
        )
        f.start()
        fourth.append(f)
    for f in fourth[len(near):]:
        f.wait_recv()
    c.wait_recv()
    for f in fourth + [c]:
        f.wait_send()
    for c in first + second + third:
        c.wait_send()


def spread_kernel(
    n_shard, mat_ref, place_ref, factor_ref, momentum_ref, gown_ref, full_ref, gall_ref,
    held, zs, zr, cs, cr, gs, gr,
):
    me, core, x, y, to_core, to_x, to_y, to_xy = place()
    z = lax.axis_index("shard")
    rows = full_ref.shape[0] // 2
    cols = full_ref.shape[1] // n_shard

    def at(side, shard):
        return (
            pl.ds(pl.multiple_of(side * rows, rows), rows),
            pl.ds(pl.multiple_of(shard * cols, cols), cols),
        )

    def nesterov(p, side):
        matrix = mat_ref[p]
        half = pl.ds(pl.multiple_of(side * rows, rows), rows)
        step = factor_ref[matrix] * gown_ref[side, place_ref[p]].astype(jnp.float32)
        new = momentum_rate * momentum_ref[matrix, half] + step
        return (step + momentum_rate * new).astype(full_ref.dtype)

    order = [d for d in (2, 1, 3) if d < n_shard] + list(range(4, n_shard))
    for d in order:
        held[d - 1] = nesterov(lax.rem(z + d, n_shard), core)
    gall_ref[me] = gown_ref[core]
    greet(
        [(p, z) for p in (to_core, to_x, to_y)]
        + [(me, lax.rem(z + d, n_shard)) for d in range(1, n_shard)]
    )
    copies = []
    for d in order:
        peer = (me, lax.rem(z + d, n_shard))
        c = remote(held.at[d - 1], full_ref.at[at(core, z)], zs.at[d - 1], zr.at[d - 1], peer)
        c.start()
        copies.append(c)
    at_g = block_at(gall_ref, 2)
    gathers = plane_gather_start(z, at_g, gs, gr)
    for side in range(2):
        full_ref[at(side, z)] = nesterov(z, side)
    onward = []
    for c, d in zip(copies, order):
        c.wait_recv()
        source = full_ref.at[at(core, lax.rem(z + n_shard - d, n_shard))]
        f = remote(source, source, cs.at[d - 1], cr.at[d - 1], (to_core, z))
        f.start()
        onward.append(f)
        if len(onward) == 1:
            plane_gather_turn(z, at_g, gs, gr, gathers)
    for f in onward:
        f.wait_recv()
    plane_gather_finish(z, at_g, gs, gr, gathers)
    for c in copies + onward:
        c.wait_send()


def newton_kernel(u_ref, o_ref):
    def total(i, carry):
        value = u_ref[pl.ds(pl.multiple_of(i * 32, 32), 32), :].astype(jnp.float32)
        return carry + jnp.sum(value * value, axis=0, keepdims=True)

    kv, width = u_ref.shape
    sums = lax.fori_loop(0, kv // 32, total, jnp.zeros((1, width), jnp.float32))
    inverse = 1.0 / (jnp.sqrt(jnp.sum(sums, axis=1, keepdims=True)) + epsilon)
    matrix = (u_ref[...].astype(jnp.float32) * inverse).astype(jnp.bfloat16)
    for iteration in range(ITERS):
        gram = lax.dot_general(
            matrix, matrix, (((1,), (1,)), ((), ())), preferred_element_type=jnp.float32
        ).astype(jnp.bfloat16)
        square = jnp.dot(gram, gram, preferred_element_type=jnp.float32)
        mixing = (coef_b * gram.astype(jnp.float32) + coef_c * square).astype(jnp.bfloat16)
        product = jnp.dot(mixing, matrix, preferred_element_type=jnp.float32)
        matrix = (coef_a * matrix.astype(jnp.float32) + product).astype(jnp.bfloat16)
    o_ref[...] = matrix


def share_kernel(
    n_shard, owner_ref, o_ref, oall_ref, whole_ref, back, bs, br, us, ur, ws, wr
):
    me, core, x, y, to_core, to_x, to_y, to_xy = place()
    z = lax.axis_index("shard")
    rows = o_ref.shape[0] // 2
    cols = o_ref.shape[1] // n_shard
    half = pl.ds(pl.multiple_of(core * rows, rows), rows)

    def piece(shard):
        return half, pl.ds(pl.multiple_of(shard * cols, cols), cols)

    peers = [(p, z) for p in (to_core, to_x, to_y)]
    peers += [(me, lax.rem(z + d, n_shard)) for d in range(1, n_shard)]
    greet(peers)
    order = [d for d in (2, 1, 3) if d < n_shard] + list(range(4, n_shard))
    returns = []
    for d in order:
        to = lax.rem(z + d, n_shard)
        c = remote(o_ref.at[piece(to)], back.at[z], bs.at[d - 1], br.at[d - 1], (me, to))
        c.start()
        returns.append(c)
    whole_ref[me] = o_ref[half]
    at_w = block_at(whole_ref, 1)
    at_u = block_at(oall_ref, 2)
    cw = plane_gather_start(z, at_w, ws, wr)
    back[z] = o_ref[piece(z)]
    for c in returns:
        c.wait_recv()
    for j in range(oall_ref.shape[1]):
        oall_ref[me, j] = back[owner_ref[j]]
    cu = plane_gather_start(z, at_u, us, ur)
    plane_gather_turn(z, at_w, ws, wr, cw)
    plane_gather_turn(z, at_u, us, ur, cu)
    plane_gather_finish(z, at_w, ws, wr, cw)
    plane_gather_finish(z, at_u, us, ur, cu)
    for c in returns:
        c.wait_send()


def finish_kernel(
    scale, block_ref, member_ref, factor_ref, slot_ref, keep_ref,
    gall_ref, oall_ref, whole_ref, momentum_ref, mout_ref, update_ref, owned_ref,
    mbuf, ubuf, wbuf, load, msem, usem, wsem,
):
    mats = mbuf.shape[0]
    slots = wbuf.shape[0]
    rows = gall_ref.shape[2]

    def fetch(m):
        return pltpu.make_async_copy(momentum_ref.at[m], mbuf.at[m], load.at[m])

    def put(buf, out, sem, m):
        return pltpu.make_async_copy(buf.at[m], out.at[m], sem.at[m])

    def each(count, body):
        def step(m, carry):
            body(m)
            return carry

        lax.fori_loop(0, count, step, 0)

    each(mats, lambda m: fetch(m).start())

    def owned_one(s):
        for c in range(2):
            value = scale * whole_ref[slot_ref[s] + c].astype(jnp.float32)
            wbuf[s, pl.ds(c * rows, rows)] = (value * keep_ref[s].astype(jnp.float32)).astype(wbuf.dtype)
        put(wbuf, owned_ref, wsem, s).start()

    def update_one(m):
        for c in range(2):
            value = oall_ref[block_ref[m] + c, member_ref[m]].astype(jnp.float32)
            ubuf[m, pl.ds(c * rows, rows)] = scale * value
        put(ubuf, update_ref, usem, m).start()

    def momentum_one(m):
        fetch(m).wait()
        for c in range(2):
            cut = pl.ds(c * rows, rows)
            step = factor_ref[m] * gall_ref[block_ref[m] + c, member_ref[m]].astype(jnp.float32)
            mbuf[m, cut] = momentum_rate * mbuf[m, cut] + step
        put(mbuf, mout_ref, msem, m).start()

    each(slots, owned_one)
    each(mats, update_one)
    each(mats, momentum_one)
    each(slots, lambda s: put(wbuf, owned_ref, wsem, s).wait())
    each(mats, lambda m: put(ubuf, update_ref, usem, m).wait())
    each(mats, lambda m: put(mbuf, mout_ref, msem, m).wait())


def per_device_planes(activations, cotangents, momentum, owners, bucket_starts):
    n_shard = lax.axis_size("shard")
    n_rep = lax.axis_size("rep")
    layers, tok_rows, width = activations.shape
    token_total = tok_rows * n_shard * n_rep
    cols = width // n_shard
    rows = KV // 2
    lanes = math.gcd(cols, 128)
    groups = n_rep // 2
    members = MATS // groups
    slots = -(-MATS // n_shard) + 1
    update_scale = math.sqrt(max(KV, D))
    bf16, f32, i32 = jnp.bfloat16, jnp.float32, jnp.int32
    shapes = [MATS] * 5 + [n_shard] * 2 + [members] + [slots] * 2
    lay, half, position, block, member, mats, places, owner, slot_block, slot_keep = pl.pallas_call(
        functools.partial(plan_kernel, n_shard, groups),
        out_shape=[jax.ShapeDtypeStruct((n,), i32) for n in shapes],
        in_specs=[SMEM_SPEC],
        out_specs=[SMEM_SPEC] * len(shapes),
        scratch_shapes=[pltpu.SMEM((MATS,), i32), pltpu.SMEM((MATS,), i32)],
        name="plan",
    )(owners)
    index = jnp.arange(MATS, dtype=i32)

    params = functools.partial(
        pltpu.CompilerParams, has_side_effects=True, vmem_limit_bytes=VMEM_LIMIT
    )
    dma = pltpu.SemaphoreType.DMA
    gown, sq = pl.pallas_call(
        functools.partial(reduce_kernel, n_shard, 1.0 / math.sqrt(token_total)),
        out_shape=(
            jax.ShapeDtypeStruct((2, members, rows, cols), bf16),
            jax.ShapeDtypeStruct((n_shard, n_rep, members, 1, lanes), f32),
        ),
        in_specs=[SMEM_SPEC, SMEM_SPEC, ANY_SPEC, ANY_SPEC],
        out_specs=(VMEM_SPEC, VMEM_SPEC),
        scratch_shapes=[
            [pltpu.VMEM((layers, 2 * tok_rows, cols), bf16) for _ in range(n_shard)],
            pltpu.VMEM((layers, 2 * tok_rows, 2 * KV), bf16),
            pltpu.VMEM((n_shard, 2, 2, members, rows, cols), bf16),
            pltpu.VMEM((n_shard, 2, members, rows, cols), bf16),
            pltpu.VMEM((n_shard, members, rows, cols), bf16),
            pltpu.VMEM((n_shard, members, rows, cols), bf16),
            pltpu.VMEM((n_shard, members, rows, cols), bf16),
            pltpu.VMEM((n_shard - 1, members, rows, cols), bf16),
            dma((n_shard + 1,)), dma((n_shard + 1,)), dma((n_shard + 1,)),
            dma((n_shard,)), dma((n_shard,)), dma((n_shard,)), dma((n_shard,)),
            dma((n_shard,)), dma((n_shard,)),
            dma((8,)), dma((8,)), dma((n_shard - 1,)), dma((n_shard - 1,)),
        ],
        compiler_params=params(collective_id=0),
        name="reduce",
    )(lay, half, activations, cotangents)

    by_position = jnp.sum(
        sq.reshape(n_shard, groups, 2, members, lanes), axis=(0, 2, 4)
    ).reshape(MATS)
    square_sums = jnp.sum(
        jnp.where(position[:, None] == index[None, :], by_position[None, :], 0.0), axis=1
    )
    factors = clip_factors(square_sums, bucket_starts)

    full, gall = pl.pallas_call(
        functools.partial(spread_kernel, n_shard),
        out_shape=(
            jax.ShapeDtypeStruct((KV, width), bf16),
            jax.ShapeDtypeStruct((n_rep, members, rows, cols), bf16),
        ),
        in_specs=[SMEM_SPEC, SMEM_SPEC, SMEM_SPEC, VMEM_SPEC, VMEM_SPEC],
        out_specs=(VMEM_SPEC, VMEM_SPEC),
        scratch_shapes=[pltpu.VMEM((n_shard - 1, rows, cols), bf16)]
        + [dma((n_shard - 1,)) for _ in range(4)]
        + [dma((10,)) for _ in range(2)],
        compiler_params=params(collective_id=1),
        name="spread",
    )(mats, places, factors, momentum, gown)

    result = pl.pallas_call(
        newton_kernel,
        out_shape=jax.ShapeDtypeStruct((KV, width), bf16),
        in_specs=[VMEM_SPEC],
        out_specs=VMEM_SPEC,
        name="newton",
    )(full)

    oall, whole = pl.pallas_call(
        functools.partial(share_kernel, n_shard),
        out_shape=(
            jax.ShapeDtypeStruct((n_rep, members, rows, cols), bf16),
            jax.ShapeDtypeStruct((n_rep, rows, width), bf16),
        ),
        in_specs=[SMEM_SPEC, VMEM_SPEC],
        out_specs=(VMEM_SPEC, VMEM_SPEC),
        scratch_shapes=[pltpu.VMEM((n_shard, rows, cols), bf16)]
        + [dma((n_shard - 1,)) for _ in range(2)]
        + [dma((10,)) for _ in range(4)],
        compiler_params=params(collective_id=2),
        name="share",
    )(owner, result)

    momentum_out, update, owned = pl.pallas_call(
        functools.partial(finish_kernel, update_scale),
        out_shape=(
            jax.ShapeDtypeStruct(momentum.shape, f32),
            jax.ShapeDtypeStruct(momentum.shape, f32),
            jax.ShapeDtypeStruct((slots, KV, width), bf16),
        ),
        in_specs=[SMEM_SPEC] * 5 + [VMEM_SPEC] * 3 + [ANY_SPEC],
        out_specs=(ANY_SPEC,) * 3,
        scratch_shapes=[
            pltpu.VMEM(momentum.shape, f32),
            pltpu.VMEM(momentum.shape, f32),
            pltpu.VMEM((slots, KV, width), bf16),
            dma((MATS,)), dma((MATS,)), dma((MATS,)), dma((slots,)),
        ],
        compiler_params=pltpu.CompilerParams(vmem_limit_bytes=VMEM_LIMIT),
        name="finish",
    )(
        block, member, factors, slot_block, slot_keep,
        gall, oall, whole, momentum,
    )
    return (momentum_out, update, owned)


def solution(mesh):
    groups = mesh.shape["rep"] // 2
    slots = -(-MATS // mesh.shape["shard"]) + 1
    fits = mesh.shape["rep"] == 8 and MATS % groups == 0 and slots <= groups
    placed = (
        P(None, ("rep", "shard"), None),
        P(None, ("rep", "shard"), None),
        P(None, None, "shard"),
        P(),
        P(),
    )
    return jax.shard_map(
        per_device_planes if fits else per_device_general,
        mesh=mesh,
        in_specs=placed,
        out_specs=(P(None, None, "shard"), P(None, None, "shard"), P("shard", None, None)),
        check_vma=False,
    )
```

profile of v0, /device:TPU:0, one launch (start us, length us, event | category | flops | bytes accessed | tf_op | source)
XLA Modules:
  0.0 177.3 jit_solution(3249654782986654238)
XLA Ops:
  0.6 0.7 fusion.2
  1.4 1.6 plan.1
  2.9 88.5 %reduce.3 = (bf16[2,3,128,512]{3,2,1,0:T(8,128)(2,1)}, f32[4,8,3,1,128]{4,3,2,1,0:T(1,128)}) custom-call(s32[12]{0:T(128)} %get-tuple-element.22.lay_ref, s32[12]{0:T(128)} %get-tuple-element.23.half_ref, bf16[6,128,2048]{2,1,0:T(8,128)(2,1)} %act_ref.1, bf16[6,128,512]{2,1,0:T(8,128)(2,1)} %cot_ref.1), custom_call_target="tpu_custom_call" | custom-call | tf_op jit(solution)/shard_map/reduce/pallas_call | solution.py:615
  91.4 0.9 reduce_sum.53
  92.4 0.1 broadcast_in_dim.14
  92.5 0.8 select_reduce_fusion
  93.3 0.2 fusion.1
  93.5 0.5 multiply_minimum_fusion.factor_ref
  94.0 24.1 %spread.1 = (bf16[256,2048]{1,0:T(8,128)(2,1)}, bf16[8,3,128,512]{3,2,1,0:T(8,128)(2,1)}) custom-call(s32[4]{0:T(128)} %get-tuple-element.27.mat_ref, s32[4]{0:T(128)} %get-tuple-element.28.place_ref, f32[12]{0:T(128)} %multiply_minimum_fusion.factor_ref, f32[12,256,512]{2,1,0:T(8,128)} %momentum_ref.3, bf16[2,3,128,512]{3,2,1,0:T(8,128)(2,1)} %get-tuple-element.29.gown_ref), custom_call_target="tpu_custom_call" | custom-call | tf_op jit(solution)/shard_map/spread/pallas_call | solution.py:649
  118.1 8.8 %newton.1.o_ref = bf16[256,2048]{1,0:T(8,128)(2,1)} custom-call(bf16[256,2048]{1,0:T(8,128)(2,1)} %get-tuple-element.32.u_ref), custom_call_target="tpu_custom_call" | custom-call | tf_op jit(solution)/shard_map/newton/pallas_call | solution.py:664
  127.0 38.5 %share.1 = (bf16[8,3,128,512]{3,2,1,0:T(8,128)(2,1)}, bf16[8,128,2048]{2,1,0:T(8,128)(2,1)}) custom-call(s32[3]{0:T(128)} %get-tuple-element.31.owner_ref, bf16[256,2048]{1,0:T(8,128)(2,1)} %newton.1.o_ref), custom_call_target="tpu_custom_call" | custom-call | tf_op jit(solution)/shard_map/share/pallas_call | solution.py:672
  165.5 11.8 %finish.1 = (f32[12,256,512]{2,1,0:T(8,128)}, f32[12,256,512]{2,1,0:T(8,128)}, bf16[4,256,2048]{2,1,0:T(8,128)(2,1)}) custom-call(s32[12]{0:T(128)} %get-tuple-element.19.block_ref, s32[12]{0:T(128)} %get-tuple-element.20.member_ref, f32[12]{0:T(128)} %multiply_minimum_fusion.factor_ref, s32[4]{0:T(128)} %get-tuple-element.25.slot_ref, ...), custom_call_target="tpu_custom_call" | custom-call | tf_op jit(solution)/shard_map/finish/pallas_call | solution.py:687
  (1 shorter events, 0.0 us)
where the time goes:
time: 178 us; the launch traced here: 177 us
  Pallas kernels  173 us (97%)
  other arithmetic  3.25 us (2%)
    pallas_call x1, Pallas kernels, per_device_planes(): pl.pallas_call(functools.partial(reduce_kernel, n_shard, 1.0 / math.sqrt(...  88.5 us
    pallas_call x1, Pallas kernels, per_device_planes(): pl.pallas_call(functools.partial(share_kernel, n_shard), out_shape=(jax.S...  38.5 us
    pallas_call x1, Pallas kernels, per_device_planes(): pl.pallas_call(functools.partial(spread_kernel, n_shard), out_shape=(jax....  24.1 us
    pallas_call x1, Pallas kernels, per_device_planes(): pl.pallas_call(functools.partial(finish_kernel, update_scale), out_shape=...  11.8 us
    pallas_call x1, Pallas kernels, per_device_planes(): pl.pallas_call(newton_kernel, out_shape=jax.ShapeDtypeStruct((KV, width),...  8.83 us

commit v1 on v0

v1 whole, which is shorter than its diff:
```python
import functools
import math

import jax
import jax.numpy as jnp
from jax import lax
from jax.experimental import pallas as pl
from jax.experimental.pallas import tpu as pltpu
from jax.sharding import PartitionSpec as P

D = 2048
KV = 256
ITERS = 5
MATS = 12
MESH = pl.DeviceIdType.MESH
VMEM_SPEC = pl.BlockSpec(memory_space=pltpu.VMEM)
SMEM_SPEC = pl.BlockSpec(memory_space=pltpu.SMEM)
ANY_SPEC = pl.BlockSpec(memory_space=pl.ANY)
VMEM_LIMIT = 60 * 1024 * 1024

coef_a = 3.4445
coef_b = -4.775
coef_c = 2.0315
momentum_rate = 0.95
clip_level = 0.5
epsilon = 1e-06


def orthogonal_batch(matrices):
    values = matrices.astype(jnp.float32)
    frobenius = jnp.sqrt(jnp.sum(values * values, axis=(1, 2), keepdims=True))
    matrix = (values / (frobenius + epsilon)).astype(jnp.bfloat16)
    for iteration in range(ITERS):
        gram_matrix = jnp.einsum(
            "skd,sjd->skj", matrix, matrix, preferred_element_type=jnp.float32
        ).astype(jnp.bfloat16)
        square = jnp.einsum(
            "skj,sji->ski", gram_matrix, gram_matrix, preferred_element_type=jnp.float32
        )
        mixing = (coef_b * gram_matrix.astype(jnp.float32) + coef_c * square).astype(jnp.bfloat16)
        product = jnp.einsum("skj,sjd->skd", mixing, matrix, preferred_element_type=jnp.float32)
        matrix = (coef_a * matrix.astype(jnp.float32) + product).astype(jnp.bfloat16)
    return matrix


def clip_factors(square_sums, bucket_starts):
    indices = jnp.arange(MATS, dtype=jnp.int32)
    buckets = jnp.sum((indices[:, None] >= bucket_starts[None, :]).astype(jnp.int32), axis=1)
    together = (buckets[:, None] == buckets[None, :]).astype(jnp.float32)
    totals = jnp.sum(together * square_sums[None, :], axis=1)
    members = jnp.sum(together, axis=1)
    root_mean = jnp.sqrt(totals / (members * KV * D) + epsilon)
    return jnp.minimum(1.0, clip_level / root_mean)


def slot_numbers(owners):
    indices = jnp.arange(MATS, dtype=jnp.int32)
    earlier = (indices[None, :] < indices[:, None]) & (owners[None, :] == owners[:, None])
    return jnp.sum(earlier.astype(jnp.int32), axis=1)


def selector(owner_of, slot_of, shard_count, slot_count):
    holders = lax.broadcasted_iota(jnp.int32, (shard_count, slot_count, 1), 0)
    places = lax.broadcasted_iota(jnp.int32, (shard_count, slot_count, 1), 1)
    chosen = (holders == owner_of[None, None, :]) & (places == slot_of[None, None, :])
    return chosen.astype(jnp.bfloat16)


def pack_slots(shards, chooser):
    return jnp.einsum("psm,mkd->skpd", chooser, shards, preferred_element_type=jnp.float32).astype(
        jnp.bfloat16
    )


def unpack_slots(received, chooser):
    return jnp.einsum("psm,skpd->mkd", chooser, received, preferred_element_type=jnp.float32)


def per_device_general(activations, cotangents, momentum, owners, bucket_starts):
    shard_count = lax.axis_size("shard")
    replica_count = lax.axis_size("rep")
    layers, tok_rows, width = activations.shape
    token_total = tok_rows * shard_count * replica_count
    columns = width // shard_count
    slot_count = -(-MATS // shard_count) + 1
    update_scale = math.sqrt(max(KV, D))
    partial_terms = jnp.einsum(
        "ltk,ltd->lkd", cotangents, activations, preferred_element_type=jnp.float32
    ).reshape(MATS, KV, width)
    shard_part = lax.psum_scatter(
        partial_terms.astype(jnp.bfloat16), "shard", scatter_dimension=2, tiled=True
    )
    summed = lax.psum(shard_part, "rep").astype(jnp.float32)
    gradient = summed / jnp.sqrt(jnp.float32(token_total))
    square_sums = lax.psum(jnp.sum(gradient * gradient, axis=(1, 2)), "shard")
    factors = clip_factors(square_sums, bucket_starts)
    momentum_out = momentum_rate * momentum + factors[:, None, None] * gradient
    nesterov = (factors[:, None, None] * gradient + momentum_rate * momentum_out).astype(
        jnp.bfloat16
    )
    slot_of = slot_numbers(owners)
    chooser = selector(owners, slot_of, shard_count, slot_count)
    received = lax.all_to_all(
        pack_slots(nesterov, chooser), "shard", split_axis=2, concat_axis=2, tiled=True
    )
    item_count = received.shape[0]
    result = orthogonal_batch(received.reshape(item_count, KV, width))
    scaled = (update_scale * result.astype(jnp.float32)).astype(jnp.bfloat16)
    returned_part = lax.all_to_all(
        result.reshape(item_count, KV, shard_count, columns),
        "shard",
        split_axis=2,
        concat_axis=2,
        tiled=True,
    )
    update = update_scale * unpack_slots(returned_part, chooser)
    return (momentum_out, update, scaled)


def lodged(block, member):
    x = lax.rem(block, 2)
    y = lax.div(block, 2)
    whole = 2 * x + y
    paired = 4 + y
    return jnp.where(member < 2, whole, paired), jnp.where(member < 2, member, x)


def lodging(matrix):
    layer = lax.div(matrix, 2)
    side = lax.rem(matrix, 2)
    early = matrix < 8
    x = jnp.where(early, lax.div(layer, 2), side)
    y = jnp.where(early, lax.rem(layer, 2), layer - 4)
    return 2 * y + x, jnp.where(early, side, 2)


def place():
    me = lax.axis_index("rep")
    core = lax.rem(me, 2)
    x = lax.rem(lax.div(me, 2), 2)
    y = lax.div(me, 4)
    to_core = me + 1 - 2 * core
    to_x = me + 2 - 4 * x
    to_y = me + 4 - 8 * y
    to_xy = me + 6 - 4 * x - 8 * y
    return me, core, x, y, to_core, to_x, to_y, to_xy


def greet(peers):
    barrier = pltpu.get_barrier_semaphore()
    for peer in peers:
        pl.semaphore_signal(barrier, inc=1, device_id=peer, device_id_type=MESH)
    pl.semaphore_wait(barrier, len(peers))


def remote(src, dst, send, recv, peer):
    return pltpu.make_async_remote_copy(
        src_ref=src, dst_ref=dst, send_sem=send, recv_sem=recv, device_id=peer, device_id_type=MESH
    )


def plane_gather_start(z, at, send, recv):
    me, core, x, y, to_core, to_x, to_y, to_xy = place()
    plan = ((0, to_x, 0), (2, to_y, 1), (1, to_x, 1), (3, to_y, 0), (4, to_core, None))
    copies = {}
    for k, peer, half in plan:
        copies[k] = remote(at(me, half), at(me, half), send.at[k], recv.at[k], (peer, z))
        copies[k].start()
    return copies


def plane_gather_turn(z, at, send, recv, copies):
    me, core, x, y, to_core, to_x, to_y, to_xy = place()

    def forward(k, block, half, peer):
        copies[k] = remote(
            at(block, half), at(block, half), send.at[k], recv.at[k], (peer, z)
        )
        copies[k].start()

    copies[0].wait_recv()
    forward(5, to_x, 0, to_y)
    copies[2].wait_recv()
    forward(6, to_y, 1, to_x)
    copies[1].wait_recv()
    forward(7, to_x, None, to_core)
    copies[3].wait_recv()
    forward(8, to_y, None, to_core)


def plane_gather_finish(z, at, send, recv, copies, last=(4, 7, 8, 9)):
    me, core, x, y, to_core, to_x, to_y, to_xy = place()
    copies[5].wait_recv()
    copies[6].wait_recv()
    copies[9] = remote(
        at(to_xy, None), at(to_xy, None), send.at[9], recv.at[9], (to_core, z)
    )
    copies[9].start()
    for k in last:
        copies[k].wait_recv()
    for k in range(10):
        copies[k].wait_send()


def reduce_kernel(
    n_shard, inverse, act_ref, cot_ref, gown_ref, sq_ref,
    act, cot, part, recv1, turn, recv2, plane, zrecv,
    local_sem, in_send, in_recv, s1, r1, s2, r2, s3, r3,
):
    me, core, x, y, to_core, to_x, to_y, to_xy = place()
    z = lax.axis_index("shard")
    tokens = act_ref.shape[1]
    rows, cols = part.shape[-2:]
    members = part.shape[2 + 1]
    steps = [d for d in (2, 1, 3) if d < n_shard] + list(range(4, n_shard)) + [0]
    peers = [(p, z) for p in (to_core, to_x, to_y)]
    peers += [(me, lax.rem(z + d, n_shard)) for d in range(1, n_shard)]
    cut = [
        pl.ds(pl.multiple_of(lax.rem(z + d, n_shard) * cols, cols), cols) for d in steps
    ]
    own = [
        pltpu.make_async_copy(
            act_ref.at[:, :, cut[k]], act[k].at[:, pl.ds(0, tokens)], local_sem.at[k]
        )
        for k in range(n_shard)
    ]
    own.append(
        pltpu.make_async_copy(cot_ref, cot.at[:, pl.ds(0, tokens)], local_sem.at[n_shard])
    )
    for c in own:
        c.start()
    greet(peers)
    theirs = pl.ds(tokens, tokens)
    swap = [
        remote(
            act_ref.at[:, :, cut[k]], act[k].at[:, theirs],
            in_send.at[k], in_recv.at[k], (to_core, z),
        )
        for k in range(n_shard)
    ]
    swap.append(
        remote(cot_ref, cot.at[:, theirs], in_send.at[n_shard], in_recv.at[n_shard], (to_core, z))
    )
    for c in swap[-1:] + swap[:-1]:
        c.start()
    for c in own:
        c.wait()
    swap[n_shard].wait()
    first = []
    second = []
    third = []

    def launch(k):
        swap[k].wait()

        def one(q, carry):
            group = lax.div(q, members)
            member = lax.rem(q, members)
            layer, side = lodged(group, member)
            block = cot[layer]
            low = jnp.where(core == 0, block[:, :rows], block[:, rows : 2 * rows])
            high = jnp.where(core == 0, block[:, 2 * rows : 3 * rows], block[:, 3 * rows :])
            left = jnp.where(side == 0, low, high)
            right = act[k][layer]
            value = lax.dot_general(
                left, right, (((0,), (0,)), ((), ())), preferred_element_type=jnp.float32
            )
            part[k, lax.div(group, 2), lax.rem(group, 2), member] = value.astype(part.dtype)
            return carry

        lax.fori_loop(0, 4 * members, one, 0)

    def send_first(k):
        if k % 2 == 0:
            c = remote(part.at[k, :, 1 - x], recv1.at[k], s1.at[k], r1.at[k], (to_x, z))
        else:
            c = remote(part.at[k, 1 - y], recv1.at[k], s1.at[k], r1.at[k], (to_y, z))
        c.start()
        first.append(c)

    def send_second(k):
        first[k].wait_recv()

        def add_out(j, carry):
            if k % 2 == 0:
                mine = part[k, 1 - y, x, j]
                came = recv1[k, 1 - y, j]
            else:
                mine = part[k, y, 1 - x, j]
                came = recv1[k, 1 - x, j]
            turn[k, j] = (mine.astype(jnp.float32) + came.astype(jnp.float32)).astype(turn.dtype)
            return carry

        lax.fori_loop(0, members, add_out, 0)
        c = remote(
            turn.at[k], recv2.at[k], s2.at[k], r2.at[k], (to_y if k % 2 == 0 else to_x, z)
        )
        c.start()
        second.append(c)

    def send_third(k):
        second[k].wait_recv()

        def add_in(j, carry):
            came = recv1[k, y, j] if k % 2 == 0 else recv1[k, x, j]
            value = part[k, y, x, j].astype(jnp.float32) + came.astype(jnp.float32)
            value = value + recv2[k, j].astype(jnp.float32)
            plane[k, j] = value.astype(plane.dtype)
            return carry

        lax.fori_loop(0, members, add_in, 0)
        if steps[k]:
            c = remote(
                plane.at[k], zrecv.at[k], s3.at[k], r3.at[k],
                (me, lax.rem(z + steps[k], n_shard)),
            )
            c.start()
            third.append(c)

    launch(0)
    send_first(0)
    launch(1)
    send_first(1)
    for k in range(2, n_shard):
        launch(k)
    for k in range(0, n_shard, 2):
        pair = [i for i in (k, k + 1) if i < n_shard]
        for i in pair:
            send_second(i)
        for i in (k + 2, k + 3):
            if i < n_shard:
                send_first(i)
        for i in pair:
            send_third(i)
    for c in third:
        c.wait_recv()

    def add_last(j, carry):
        value = plane[n_shard - 1, j].astype(jnp.float32)
        for k in range(n_shard - 1):
            value = value + zrecv[k, j].astype(jnp.float32)
        value = (value * inverse).astype(gown_ref.dtype)
        gown_ref[j] = value
        value = value.astype(jnp.float32)
        line = jnp.sum(value * value, axis=0, keepdims=True)
        lanes = sq_ref.shape[-1]
        fold = line[:, :lanes]
        for i in range(1, cols // lanes):
            fold = fold + line[:, i * lanes : (i + 1) * lanes]
        sq_ref[j] = fold
        return carry

    lax.fori_loop(0, members, add_last, 0)
    for c in first + second + third:
        c.wait_send()


HOMES = ((1, 0), (2, 0), (2, 1))


def block_at(ref, axis, rows):
    def at(r, half):
        count = rows if half is None else rows // 2
        start = lax.rem(r, 2) * rows + (0 if half is None else half * count)
        cut = pl.ds(pl.multiple_of(start, count), count)
        block = lax.div(r, 2)
        return ref.at[block, cut] if axis == 1 else ref.at[block, :, cut]

    return at


def split(value):
    high = value.astype(jnp.bfloat16)
    return high, (value - high.astype(jnp.float32)).astype(jnp.bfloat16)


def times(left, right):
    dot = functools.partial(jnp.dot, preferred_element_type=jnp.float32)
    return dot(left[0], right[0]) + (dot(left[0], right[1]) + dot(left[1], right[0]))


def gram_iteration(gram, scale, gram_scr, root_scr):
    n = gram.shape[0]
    row = lax.broadcasted_iota(jnp.int32, (n, n), 0)
    col = lax.broadcasted_iota(jnp.int32, (n, n), 1)
    eye = (row == col).astype(jnp.float32)
    trace = jnp.sum(jnp.sum(gram * eye, axis=0, keepdims=True), axis=1, keepdims=True)
    inverse = 1.0 / (jnp.sqrt(trace) + epsilon)
    gram_scr[...] = gram * inverse * inverse
    for iteration in range(ITERS):
        a = split(gram_scr[...])
        mixing = coef_b * gram_scr[...] + coef_c * times(a, a)
        b = split(mixing)
        if iteration == 0:
            root_scr[...] = coef_a * eye + mixing
        else:
            root_scr[...] = coef_a * root_scr[...] + times(b, split(root_scr[...]))
        if iteration < ITERS - 1:
            half = coef_a * gram_scr[...] + times(b, a)
            gram_scr[...] = coef_a * half + times(b, split(half))
    return root_scr[...] * (inverse * scale)


def settle_kernel(
    n_shard, scale, owner_ref, start_ref, momentum_hbm, gown_ref, sq_ref,
    mout_ref, u_ref, wall_ref, qall_ref,
    momentum, gall, sqall, table, factor, uown, held, gram_out, gram_in, gram_scr, root_scr, root,
    load, ps, pr, qs, qr, gs, gr, as_, ar, ws, wr, os_, or_, rs, rr, hs, hr,
):
    f32, bf16 = jnp.float32, jnp.bfloat16
    me, core, x, y, to_core, to_x, to_y, to_xy = place()
    z = lax.axis_index("shard")
    base = me - core
    block = lax.div(me, 2)
    members, rows, cols = gown_ref.shape
    lanes = sq_ref.shape[-1]
    other = 1 - 2 * core
    near = (to_core, to_x, to_y, to_xy, to_x + other, to_y + other, to_xy + other)
    mine = pl.ds(pl.multiple_of(core * rows, rows), rows)

    fetch = pltpu.make_async_copy(momentum_hbm, momentum, load)
    fetch.start()
    column = [(base + c, lax.rem(z + d, n_shard)) for d in range(1, n_shard) for c in range(2)]
    greet([(p, z) for p in near] + column)

    sqall[0, me] = sq_ref[...]
    squares = []
    for k, peer in enumerate(near):
        c = remote(sqall.at[0, me], sqall.at[0, me], ps.at[k], pr.at[k], (peer, z))
        c.start()
        squares.append(c)
    gall[block, :, mine] = gown_ref[...]
    at_g = block_at(gall, 2, rows)
    gathers = plane_gather_start(z, at_g, gs, gr)
    for c in squares:
        c.wait_recv()
    lines = []
    for d in range(1, n_shard):
        c = remote(sqall.at[0], sqall.at[d], qs.at[d - 1], qr.at[d - 1], (me, lax.rem(z + d, n_shard)))
        c.start()
        lines.append(c)
    fetch.wait()
    for c in lines:
        c.wait_recv()

    table[...] = jnp.zeros_like(table)
    for m in range(MATS):
        layer, side = divmod(m, 2)
        bx, by = divmod(layer, 2) if m < 8 else (side, layer - 4)
        j, i = 2 * by + bx, side if m < 8 else 2
        line = sqall[0, 2 * j, i] + sqall[0, 2 * j + 1, i]
        for d in range(1, n_shard):
            line = line + sqall[d, 2 * j, i] + sqall[d, 2 * j + 1, i]
        table[pl.ds(m, 1)] = line
    index = lax.broadcasted_iota(jnp.int32, table.shape, 0)
    bucket = jnp.zeros(table.shape, jnp.int32)
    for k in range(start_ref.shape[0]):
        bucket = bucket + (index >= start_ref[k]).astype(jnp.int32)
    sums = table[...]
    clip = jnp.zeros(table.shape, f32)
    for k in range(start_ref.shape[0] + 1):
        inside = (bucket == k) & (index < MATS)
        total = jnp.sum(jnp.where(inside, sums, 0.0), axis=(0, 1), keepdims=True)
        count = jnp.sum(inside.astype(f32), axis=(0, 1), keepdims=True) / lanes
        mean = total / (jnp.maximum(count, 1.0) * (2 * rows) * (n_shard * cols))
        clip = jnp.where(inside, jnp.minimum(1.0, clip_level / jnp.sqrt(mean + epsilon)), clip)
    for m in range(MATS):
        factor[m] = jnp.concatenate([clip[m : m + 1, :]] * (cols // lanes), axis=1)

    def advance(matrix, gradient, past):
        step = factor[matrix] * gradient.astype(f32)
        new = momentum_rate * past + step
        return new, (step + momentum_rate * new).astype(bf16)

    gathers[4].wait_recv()
    for i in range(members):
        layer, side = lodged(block, i)
        matrix = 2 * layer + side
        uown[i] = advance(matrix, gall[block, i], momentum[matrix])[1]
    over = (((1,), (1,)), ((), ()))
    parts = []
    for i, (hz, hc) in enumerate(HOMES):
        here = (z == hz) & (core == hc)
        owner = (base + hc, hz)
        low = uown[i, :rows]
        high = uown[i, rows:]
        own = jnp.where(core == 0, low, high)
        diag = lax.dot_general(own, own, over, preferred_element_type=f32)
        gram_out[i, 0] = diag
        part = remote(gram_out.at[i, 0], gram_in.at[z, core], as_.at[i, 0], ar.at[z, core], owner)
        cross = remote(gram_out.at[i, 1], gram_in.at[z, 2], as_.at[i, 1], ar.at[z, 2], owner)
        parts.append((here, part, cross))

        @pl.when(here)
        def _():
            gram_in[z, core] = diag

        @pl.when(jnp.logical_not(here))
        def _():
            part.start()

        @pl.when(core == 0)
        def _():
            off = lax.dot_general(low, high, over, preferred_element_type=f32)
            gram_out[i, 1] = off

            @pl.when(here)
            def _():
                gram_in[z, 2] = off

            @pl.when(jnp.logical_not(here))
            def _():
                cross.start()

    plane_gather_turn(z, at_g, gs, gr, gathers)
    plane_gather_finish(z, at_g, gs, gr, gathers, last=(7, 8, 9))

    def slot_matrix(shard, slot):
        found = jnp.int32(0)
        count = jnp.int32(0)
        for m in range(MATS):
            yes = owner_ref[m] == shard
            found = jnp.where(yes & (count == slot), m, found)
            count = count + yes.astype(jnp.int32)
        return found

    sends = []
    for d in (1, 3, 2):
        shard = lax.rem(z + d, n_shard)
        matrix = slot_matrix(shard, block)
        home, member = lodging(matrix)
        held[d - 1] = advance(matrix, gall[home, member, mine], momentum[matrix, mine])[1]
        c = remote(
            held.at[d - 1], wall_ref.at[n_shard - d - 1, block, mine],
            ws.at[d - 1], wr.at[d - 1], (me, shard),
        )
        c.start()
        sends.append((d, c))

    def all_one(m, carry):
        home, member = lodging(m)
        new, turned = advance(m, gall[home, member], momentum[m])
        mout_ref[m] = new
        u_ref[m] = turned
        return carry

    lax.fori_loop(0, MATS, all_one, 0)

    is_home = functools.reduce(jnp.logical_or, [here for here, _, _ in parts])
    member = jnp.where(z == HOMES[0][0], 0, 1 + core)
    roots = []
    for d in range(n_shard):
        for c in range(2):
            if d == 0 and c == 1:
                continue
            peer = (to_core, z) if d == 0 else (base + c, lax.rem(z + d, n_shard))
            half = 1 - core if d == 0 else c
            cut = pl.ds(pl.multiple_of(half * rows, rows), rows)
            k = len(roots)
            roots.append(remote(root.at[cut], qall_ref.at[block, member, cut], rs.at[k], rr.at[member], peer))

    @pl.when(is_home)
    def _():
        for d in range(n_shard):
            for k in range(3):
                source = remote(gram_out.at[0, 0], gram_in.at[d, k], as_.at[0, 0], ar.at[d, k], (to_core, z))
                local = (z == d) & ((core == k) if k < 2 else (core == 0))

                @pl.when(jnp.logical_not(local))
                def _():
                    source.wait_recv()

        blocks = []
        for k in range(3):
            value = gram_in[0, k]
            for d in range(1, n_shard):
                value = value + gram_in[d, k]
            blocks.append(value)
        top = jnp.concatenate([blocks[0], blocks[2]], axis=1)
        bottom = jnp.concatenate([blocks[2].T, blocks[1]], axis=1)
        result = gram_iteration(jnp.concatenate([top, bottom], axis=0), scale, gram_scr, root_scr)
        root[...] = result.astype(bf16)
        for c in roots:
            c.start()
        qall_ref[block, member, mine] = root[mine]

    at_w = {d: block_at(wall_ref.at[n_shard - d - 1], 1, rows) for d, _ in sends}
    walls = {}
    for d, c in sends:
        c.wait_recv()
        walls[d] = plane_gather_start(z, at_w[d], os_.at[d - 1], or_.at[d - 1])
    order = [d for d, _ in sends]
    plane_gather_turn(z, at_w[order[0]], os_.at[order[0] - 1], or_.at[order[0] - 1], walls[order[0]])
    for i, (here, _, _) in enumerate(parts):
        arrival = remote(root.at[mine], qall_ref.at[block, i, mine], rs.at[0], rr.at[i], (to_core, z))

        @pl.when(jnp.logical_not(here))
        def _():
            arrival.wait_recv()

    at_q = block_at(qall_ref, 2, rows)
    gathers_q = plane_gather_start(z, at_q, hs, hr)
    for d in order[1:]:
        plane_gather_turn(z, at_w[d], os_.at[d - 1], or_.at[d - 1], walls[d])
    plane_gather_turn(z, at_q, hs, hr, gathers_q)
    for d in order:
        plane_gather_finish(z, at_w[d], os_.at[d - 1], or_.at[d - 1], walls[d])
    plane_gather_finish(z, at_q, hs, hr, gathers_q)

    @pl.when(is_home)
    def _():
        for c in roots:
            c.wait_send()

    for here, part, cross in parts:

        @pl.when(jnp.logical_not(here))
        def _():
            part.wait_send()

            @pl.when(core == 0)
            def _():
                cross.wait_send()

    for _, c in sends:
        c.wait_send()
    for c in squares + lines:
        c.wait_send()


def finish_kernel(
    owner_ref, mout_ref, u_ref, wall_ref, qall_ref, mom_out, update_out, owned_out,
    ubuf, wbuf, msem, usem, wsem,
):
    f32 = jnp.float32
    slots, _, width = wbuf.shape
    mats, _, cols = ubuf.shape
    n_shard = width // cols
    z = lax.axis_index("shard")
    whole = pltpu.make_async_copy(mout_ref, mom_out, msem)
    whole.start()

    def put(buf, out, sem, m):
        return pltpu.make_async_copy(buf.at[m], out.at[m], sem.at[m])

    def update_one(m, carry):
        home, member = lodging(m)
        ubuf[m] = jnp.dot(qall_ref[home, member], u_ref[m], preferred_element_type=f32)
        put(ubuf, update_out, usem, m).start()
        return carry

    lax.fori_loop(0, mats, update_one, 0)

    def owned_one(s, carry):
        matrix = jnp.int32(0)
        count = jnp.int32(0)
        for m in range(mats):
            yes = owner_ref[m] == z
            matrix = jnp.where(yes & (count == s), m, matrix)
            count = count + yes.astype(jnp.int32)
        keep = (count > s).astype(f32)
        home, member = lodging(matrix)
        q = qall_ref[home, member]
        for d in range(n_shard):
            right = u_ref[matrix] if d == 0 else wall_ref[d - 1, s]
            value = jnp.dot(q, right, preferred_element_type=f32) * keep
            at = lax.rem(z + d, n_shard)
            wbuf[s, :, pl.ds(pl.multiple_of(at * cols, cols), cols)] = value.astype(wbuf.dtype)
        put(wbuf, owned_out, wsem, s).start()
        return carry

    lax.fori_loop(0, slots, owned_one, 0)

    def each(count, buf, out, sem):
        def step(m, carry):
            put(buf, out, sem, m).wait()
            return carry

        lax.fori_loop(0, count, step, 0)

    whole.wait()
    each(mats, ubuf, update_out, usem)
    each(slots, wbuf, owned_out, wsem)


def per_device_planes(activations, cotangents, momentum, owners, bucket_starts):
    n_shard = lax.axis_size("shard")
    n_rep = lax.axis_size("rep")
    layers, tok_rows, width = activations.shape
    token_total = tok_rows * n_shard * n_rep
    cols = width // n_shard
    rows = KV // 2
    lanes = math.gcd(cols, 128)
    groups = n_rep // 2
    members = MATS // groups
    slots = -(-MATS // n_shard) + 1
    update_scale = math.sqrt(max(KV, D))
    bf16, f32 = jnp.bfloat16, jnp.float32

    def params(limit, **rest):
        return pltpu.CompilerParams(vmem_limit_bytes=limit * 1024 * 1024, **rest)

    dma = pltpu.SemaphoreType.DMA
    gown, sq = pl.pallas_call(
        functools.partial(reduce_kernel, n_shard, 1.0 / math.sqrt(token_total)),
        out_shape=(
            pltpu.VMEM((members, rows, cols), bf16),
            pltpu.VMEM((members, 1, lanes), f32),
        ),
        in_specs=[ANY_SPEC, ANY_SPEC],
        out_specs=(VMEM_SPEC, VMEM_SPEC),
        scratch_shapes=[
            [pltpu.VMEM((layers, 2 * tok_rows, cols), bf16) for _ in range(n_shard)],
            pltpu.VMEM((layers, 2 * tok_rows, 2 * KV), bf16),
            pltpu.VMEM((n_shard, 2, 2, members, rows, cols), bf16),
            pltpu.VMEM((n_shard, 2, members, rows, cols), bf16),
            pltpu.VMEM((n_shard, members, rows, cols), bf16),
            pltpu.VMEM((n_shard, members, rows, cols), bf16),
            pltpu.VMEM((n_shard, members, rows, cols), bf16),
            pltpu.VMEM((n_shard - 1, members, rows, cols), bf16),
            dma((n_shard + 1,)), dma((n_shard + 1,)), dma((n_shard + 1,)),
            dma((n_shard,)), dma((n_shard,)), dma((n_shard,)), dma((n_shard,)),
            dma((n_shard,)), dma((n_shard,)),
        ],
        compiler_params=params(44, has_side_effects=True, collective_id=0),
        name="reduce",
    )(activations, cotangents)

    mout, turned, wall, qall = pl.pallas_call(
        functools.partial(settle_kernel, n_shard, update_scale),
        out_shape=(
            pltpu.VMEM((MATS, KV, cols), f32),
            pltpu.VMEM((MATS, KV, cols), bf16),
            pltpu.VMEM((n_shard - 1, slots, KV, cols), bf16),
            pltpu.VMEM((groups, members, KV, KV), bf16),
        ),
        in_specs=[SMEM_SPEC, SMEM_SPEC, ANY_SPEC, VMEM_SPEC, VMEM_SPEC],
        out_specs=(VMEM_SPEC,) * 4,
        scratch_shapes=[
            pltpu.VMEM((MATS, KV, cols), f32),
            pltpu.VMEM((groups, members, KV, cols), bf16),
            pltpu.VMEM((n_shard, n_rep, members, 1, lanes), f32),
            pltpu.VMEM((16, lanes), f32),
            pltpu.VMEM((MATS, 1, cols), f32),
            pltpu.VMEM((members, KV, cols), bf16),
            pltpu.VMEM((n_shard - 1, rows, cols), bf16),
            pltpu.VMEM((members, 2, rows, rows), f32),
            pltpu.VMEM((n_shard, 3, rows, rows), f32),
            pltpu.VMEM((KV, KV), f32),
            pltpu.VMEM((KV, KV), f32),
            pltpu.VMEM((KV, KV), bf16),
            dma(()),
            dma((7,)), dma((7,)), dma((n_shard - 1,)), dma((n_shard - 1,)),
            dma((10,)), dma((10,)),
            dma((members, 2)), dma((n_shard, 3)),
            dma((n_shard - 1,)), dma((n_shard - 1,)),
            dma((n_shard - 1, 10)), dma((n_shard - 1, 10)),
            dma((2 * n_shard - 1,)), dma((members,)),
            dma((10,)), dma((10,)),
        ],
        compiler_params=params(32, has_side_effects=True, collective_id=1),
        name="settle",
    )(owners, bucket_starts, momentum, gown, sq)

    return pl.pallas_call(
        finish_kernel,
        out_shape=(
            jax.ShapeDtypeStruct(momentum.shape, f32),
            jax.ShapeDtypeStruct(momentum.shape, f32),
            jax.ShapeDtypeStruct((slots, KV, width), bf16),
        ),
        in_specs=[SMEM_SPEC] + [VMEM_SPEC] * 4,
        out_specs=(ANY_SPEC,) * 3,
        scratch_shapes=[
            pltpu.VMEM(momentum.shape, f32),
            pltpu.VMEM((slots, KV, width), bf16),
            dma(()), dma((MATS,)), dma((slots,)),
        ],
        compiler_params=params(20),
        name="finish",
    )(owners, mout, turned, wall, qall)


def solution(mesh):
    groups = mesh.shape["rep"] // 2
    slots = -(-MATS // mesh.shape["shard"]) + 1
    fits = mesh.shape["rep"] == 8 and mesh.shape["shard"] == 4 and slots <= groups
    placed = (
        P(None, ("rep", "shard"), None),
        P(None, ("rep", "shard"), None),
        P(None, None, "shard"),
        P(),
        P(),
    )
    return jax.shard_map(
        per_device_planes if fits else per_device_general,
        mesh=mesh,
        in_specs=placed,
        out_specs=(P(None, None, "shard"), P(None, None, "shard"), P("shard", None, None)),
        check_vma=False,
    )
```

time: 178 us -> 145 us (0.81)
  Pallas kernels: 173 us -> 137 us
  local copies, waits for them, and re-layouts: 0.09 us -> 7.1 us
  other arithmetic: 3.25 us -> 0 us
    pallas_call x5 -> x2, Pallas kernels: 84.8 us -> 58 us  [the longest x1 51.4 us: per_device_planes(): pl.pallas_call(functools.partial(settle_kernel, n_shard, update_scale), o...]
    pallas_call x1, Pallas kernels: 88.5 us -> 79 us  [per_device_planes(): pl.pallas_call(functools.partial(reduce_kernel, n_shard, 1.0 / math.sqrt(...]
    unnamed x0 -> x10, local copies, waits for them, and re-layouts: none -> 7.1 us
    reduce_sum x5 -> x0, other arithmetic: 2.72 us -> none  [the longest x2 0.96 us: per_device_planes(): jnp.sum(sq.reshape(n_shard, groups, 2, members, lanes), axis=(0, 2, 4))]
where the time goes in v1:
time: 145 us
  Pallas kernels  137 us (94%)
  local copies, waits for them, and re-layouts  7.1 us (5%)
    pallas_call x1, Pallas kernels, per_device_planes(): pl.pallas_call(functools.partial(reduce_kernel, n_shard, 1.0 / math.sqrt(...  79 us
    pallas_call x1, Pallas kernels, per_device_planes(): pl.pallas_call(functools.partial(settle_kernel, n_shard, update_scale), o...  51.4 us
    unnamed x10, local copies, waits for them, and re-layouts  7.1 us
    pallas_call x1, Pallas kernels, per_device_planes(): pl.pallas_call(finish_kernel, out_shape=(jax.ShapeDtypeStruct(momentum.sh...  6.57 us

profile of v1, /device:TPU:0, one launch (start us, length us, event | category | flops | bytes accessed | tf_op | source)
XLA Modules:
  0.0 144.8 jit_solution(3721938622629238976)
XLA Ops:
  0.6 0.0 copy-start.1
  0.6 1.9 %copy-done.1 = bf16[6,128,2048]{2,1,0:T(8,128)(2,1)S(1)} copy-done((bf16[6,128,2048]{2,1,0:T(8,128)(2,1)S(1)}, bf16[6,128,2048]{2,1,0:T(8,128)(2,1)}, u32[]{:S(2)}) %copy-start.1) | copy-done | bytes 3145752
  2.5 0.0 copy-start.2
  2.5 1.1 copy-done.2
  3.7 79.0 %reduce.1 = (bf16[3,128,512]{2,1,0:T(8,128)(2,1)S(1)}, f32[3,1,128]{2,1,0:T(1,128)S(1)}) custom-call(bf16[6,128,2048]{2,1,0:T(8,128)(2,1)S(1)} %copy-done.1, bf16[6,128,512]{2,1,0:T(8,128)(2,1)S(1)} %copy-done.2), custom_call_target="tpu_custom_call" | custom-call | tf_op jit(solution)/shard_map/reduce/pallas_call | solution.py:704
  82.7 0.0 copy-start
  82.7 2.8 %copy-done = f32[12,256,512]{2,1,0:T(8,128)S(1)} copy-done((f32[12,256,512]{2,1,0:T(8,128)S(1)}, f32[12,256,512]{2,1,0:T(8,128)}, u32[]{:S(2)}) %copy-start) | copy-done | bytes 6291480
  85.5 0.0 copy-start.3
  85.5 0.7 copy-done.3
  86.1 0.0 copy-start.4
  86.1 0.7 copy-done.4
  86.8 51.4 %settle.1 = (f32[12,256,512]{2,1,0:T(8,128)S(1)}, bf16[12,256,512]{2,1,0:T(8,128)(2,1)S(1)}, bf16[3,4,256,512]{3,2,1,0:T(8,128)(2,1)S(1)}, bf16[4,3,256,256]{3,2,1,0:T(8,128)(2,1)S(1)}) custom-call(s32[12]{0:T(128)S(1)} %copy-done.3, s32[2]{0:T(128)S(1)} %copy-done.4, f32[12,256,512]{2,1,0:T(8,128)S(1)} %copy-done, ...), custom_call_target="tpu_custom_call" | custom-call | tf_op jit(solution)/shard_map/settle/pallas_call | solution.py:729
  138.2 6.6 %finish.1 = (f32[12,256,512]{2,1,0:T(8,128)}, f32[12,256,512]{2,1,0:T(8,128)}, bf16[4,256,2048]{2,1,0:T(8,128)(2,1)}) custom-call(s32[12]{0:T(128)S(1)} %copy-done.3, f32[12,256,512]{2,1,0:T(8,128)S(1)} %get-tuple-element.11.mout_ref, bf16[12,256,512]{2,1,0:T(8,128)(2,1)S(1)} %get-tuple-element.12.u_ref, ...), custom_call_target="tpu_custom_call" | custom-call | tf_op jit(solution)/shard_map/finish/pallas_call | solution.py:765
Async XLA Ops:
  0.6 1.9 %copy-start.1 = (bf16[6,128,2048]{2,1,0:T(8,128)(2,1)S(1)}, bf16[6,128,2048]{2,1,0:T(8,128)(2,1)}, u32[]{:S(2)}) copy-start(bf16[6,128,2048]{2,1,0:T(8,128)(2,1)} %act_ref.1) | copy-start | bytes 9437188
  2.5 1.1 copy-start.2
  82.7 2.8 %copy-start = (f32[12,256,512]{2,1,0:T(8,128)S(1)}, f32[12,256,512]{2,1,0:T(8,128)}, u32[]{:S(2)}) copy-start(f32[12,256,512]{2,1,0:T(8,128)} %momentum_hbm.1) | copy-start | bytes 18874372
  85.5 0.7 copy-start.3
  86.1 0.7 copy-start.4

commit v2 on v1

--- a/solution.py
+++ b/solution.py
@@ -202,157 +202,213 @@
         copies[k].wait_send()
 
 
-def reduce_kernel(
-    n_shard, inverse, act_ref, cot_ref, gown_ref, sq_ref,
-    act, cot, part, recv1, turn, recv2, plane, zrecv,
-    local_sem, in_send, in_recv, s1, r1, s2, r2, s3, r3,
+def gather_reduce(
+    n_shard, inverse, act_ref, cot_ref, gall, sqall, act, cot, turned, part, recv, plane, far, zrecv,
+    own_sem, swap_s, swap_r, hop_s, hop_r, pass_s, pass_r, sum_s, sum_r, line_s, line_r,
 ):
+    f32 = jnp.float32
     me, core, x, y, to_core, to_x, to_y, to_xy = place()
     z = lax.axis_index("shard")
     tokens = act_ref.shape[1]
-    rows, cols = part.shape[-2:]
-    members = part.shape[2 + 1]
-    steps = [d for d in (2, 1, 3) if d < n_shard] + list(range(4, n_shard)) + [0]
-    peers = [(p, z) for p in (to_core, to_x, to_y)]
-    peers += [(me, lax.rem(z + d, n_shard)) for d in range(1, n_shard)]
-    cut = [
-        pl.ds(pl.multiple_of(lax.rem(z + d, n_shard) * cols, cols), cols) for d in steps
-    ]
-    own = [
-        pltpu.make_async_copy(
-            act_ref.at[:, :, cut[k]], act[k].at[:, pl.ds(0, tokens)], local_sem.at[k]
+    members, rows, cols = plane.shape[1:]
+    near = z + 1 - 2 * lax.rem(z, 2)
+    across = z + 2 - 4 * lax.div(z, 2)
+    targets = (n_shard - 1 - z, across, near, z)
+    cut = [pl.ds(pl.multiple_of(t * cols, cols), cols) for t in targets]
+    counts = [c.shape[0] for c in cot]
+    shared = counts[0] * 2
+    mine = (counts[0] * x, shared + counts[1] * y)
+    yours = (counts[0] * (1 - x), shared + counts[1] * (1 - y))
+    peers = (to_x, to_y)
+    waits = []
+
+    def source(kind, k, layer):
+        span = pl.ds(layer, counts[kind])
+        return cot_ref.at[span] if k == n_shard else act_ref.at[span, :, cut[k]]
+
+    def slot(kind, k, s):
+        buffer = cot[kind] if k == n_shard else act[kind].at[k]
+        return buffer.at[:, pl.ds(s * tokens, tokens)]
+
+    order = [(1, n_shard), (0, n_shard)] + [(kind, k) for k in range(n_shard) for kind in (1, 0)]
+    own = {
+        (kind, k): pltpu.make_async_copy(
+            source(kind, k, mine[kind]), slot(kind, k, 0), own_sem.at[kind, k]
         )
+        for kind, k in order
+    }
+    swap = {
+        (kind, k): remote(
+            source(kind, k, mine[kind]), slot(kind, k, 1),
+            swap_s.at[kind, k], swap_r.at[kind, k], (to_core, z),
+        )
+        for kind, k in order
+    }
+    hop = {
+        (kind, k): remote(
+            source(kind, k, yours[kind]), slot(kind, k, 2),
+            hop_s.at[kind, k], hop_r.at[kind, k], (peers[kind], z),
+        )
+        for kind, k in order
+    }
+    onward = {
+        (kind, k): remote(
+            slot(kind, k, 2), slot(kind, k, 3),
+            pass_s.at[kind, k], pass_r.at[kind, k], (to_core, z),
+        )
+        for kind, k in order
+    }
+    sums = [
+        [
+            remote(
+                part[0].at[k, 1 - y], recv[0].at[k],
+                sum_s.at[0, k], sum_r.at[0, k], (to_y, z),
+            ),
+            remote(
+                part[1].at[k, 1 - x], recv[1].at[k],
+                sum_s.at[1, k], sum_r.at[1, k], (to_x, z),
+            ),
+        ]
         for k in range(n_shard)
     ]
-    own.append(
-        pltpu.make_async_copy(cot_ref, cot.at[:, pl.ds(0, tokens)], local_sem.at[n_shard])
-    )
-    for c in own:
-        c.start()
-    greet(peers)
-    theirs = pl.ds(tokens, tokens)
-    swap = [
-        remote(
-            act_ref.at[:, :, cut[k]], act[k].at[:, theirs],
-            in_send.at[k], in_recv.at[k], (to_core, z),
-        )
-        for k in range(n_shard)
+    spans = (pl.ds(0, members - 1), pl.ds(members - 1, 1))
+    lines = [
+        [
+            remote(
+                (far if m == 1 else plane.at[m]).at[spans[kind]], zrecv.at[m, spans[kind]],
+                line_s.at[m, kind], line_r.at[m, kind], (me, across if m == 1 else near),
+            )
+            for kind in range(2)
+        ]
+        for m in range(n_shard - 1)
     ]
-    swap.append(
-        remote(cot_ref, cot.at[:, theirs], in_send.at[n_shard], in_recv.at[n_shard], (to_core, z))
-    )
-    for c in swap[-1:] + swap[:-1]:
-        c.start()
-    for c in own:
-        c.wait()
-    swap[n_shard].wait()
-    first = []
-    second = []
-    third = []
-
-    def launch(k):
-        swap[k].wait()
+
+    def enter():
+        for key in order:
+            own[key].start()
+
+    def begin():
+        for key in order:
+            if key != (0, n_shard - 1):
+                hop[key].start()
+        for key in order:
+            swap[key].start()
+
+    def take(kind, k):
+        hop[kind, k].wait_recv()
+        onward[kind, k].start()
+
+    def ready(kind, k):
+        own[kind, k].wait()
+        swap[kind, k].wait_recv()
+        onward[kind, k].wait_recv()
+
+    def turn(kind):
+        ready(kind, n_shard)
+        for layer in range(counts[kind]):
+            for side in range(2):
+                at = pl.ds(pl.multiple_of((2 * side + core) * rows, rows), rows)
+                turned[kind][layer, side] = cot[kind][layer, :, at].T
+
+    def product(kind, k):
+        ready(kind, k)
 
         def one(q, carry):
-            group = lax.div(q, members)
-            member = lax.rem(q, members)
-            layer, side = lodged(group, member)
-            block = cot[layer]
-            low = jnp.where(core == 0, block[:, :rows], block[:, rows : 2 * rows])
-            high = jnp.where(core == 0, block[:, 2 * rows : 3 * rows], block[:, 3 * rows :])
-            left = jnp.where(side == 0, low, high)
-            right = act[k][layer]
-            value = lax.dot_general(
-                left, right, (((0,), (0,)), ((), ())), preferred_element_type=jnp.float32
-            )
-            part[k, lax.div(group, 2), lax.rem(group, 2), member] = value.astype(part.dtype)
+            layer = lax.div(q, 2)
+            side = lax.rem(q, 2)
+            value = jnp.dot(turned[kind][layer, side], act[kind][k, layer], preferred_element_type=f32)
+            if kind == 0:
+                part[0][k, layer, side] = value.astype(part[0].dtype)
+            else:
+                part[1][k, side, 0] = value.astype(part[1].dtype)
             return carry
 
-        lax.fori_loop(0, 4 * members, one, 0)
-
-    def send_first(k):
-        if k % 2 == 0:
-            c = remote(part.at[k, :, 1 - x], recv1.at[k], s1.at[k], r1.at[k], (to_x, z))
-        else:
-            c = remote(part.at[k, 1 - y], recv1.at[k], s1.at[k], r1.at[k], (to_y, z))
-        c.start()
-        first.append(c)
-
-    def send_second(k):
-        first[k].wait_recv()
-
-        def add_out(j, carry):
-            if k % 2 == 0:
-                mine = part[k, 1 - y, x, j]
-                came = recv1[k, 1 - y, j]
-            else:
-                mine = part[k, y, 1 - x, j]
-                came = recv1[k, 1 - x, j]
-            turn[k, j] = (mine.astype(jnp.float32) + came.astype(jnp.float32)).astype(turn.dtype)
+        lax.fori_loop(0, 2 * counts[kind], one, 0)
+        sums[k][kind].start()
+
+    def gather(kind, k):
+        sums[k][kind].wait_recv()
+        for i in range(members - 1 if kind == 0 else 1):
+            kept = part[0][k, y, i] if kind == 0 else part[1][k, x, i]
+            value = kept.astype(f32) + recv[kind][k, i].astype(f32)
+            plane[k, i if kind == 0 else members - 1] = value.astype(plane.dtype)
+
+    def cross(kind):
+        lines[0][kind].wait_recv()
+        for i in range(members - 1) if kind == 0 else (members - 1,):
+            value = plane[1, i].astype(f32) + zrecv[0, i].astype(f32)
+            far[i] = value.astype(far.dtype)
+        lines[1][kind].start()
+
+    def run():
+        take(1, n_shard)
+        take(1, 0)
+        take(0, n_shard)
+        turn(1)
+        product(1, 0)
+        take(1, 1)
+        turn(0)
+        product(1, 1)
+        hop[0, n_shard - 1].start()
+        take(0, 0)
+        take(1, 2)
+        product(0, 0)
+        product(1, 2)
+        take(1, 3)
+        product(1, 3)
+        take(0, 1)
+        product(0, 1)
+        gather(0, 0)
+        lines[0][0].start()
+        take(0, 2)
+        product(0, 2)
+        gather(1, 0)
+        lines[0][1].start()
+        gather(0, 1)
+        gather(1, 1)
+        cross(0)
+        cross(1)
+        gather(0, 2)
+        lines[2][0].start()
+        take(0, 3)
+        product(0, 3)
+        gather(1, 2)
+        lines[2][1].start()
+        gather(1, 3)
+        gather(0, 3)
+        for m in (2, 1):
+            for c in lines[m]:
+                c.wait_recv()
+        home = lax.div(me, 2)
+        half = pl.ds(pl.multiple_of(core * rows, rows), rows)
+
+        def add_last(j, carry):
+            value = plane[n_shard - 1, j].astype(f32)
+            for m in (1, 2):
+                value = value + zrecv[m, j].astype(f32)
+            value = (value * inverse).astype(gall.dtype)
+            gall[home, j, half] = value
+            value = value.astype(f32)
+            line = jnp.sum(value * value, axis=0, keepdims=True)
+            lanes = sqall.shape[-1]
+            fold = line[:, :lanes]
+            for i in range(1, cols // lanes):
+                fold = fold + line[:, i * lanes : (i + 1) * lanes]
+            sqall[0, me, j] = fold
             return carry
 
-        lax.fori_loop(0, members, add_out, 0)
-        c = remote(
-            turn.at[k], recv2.at[k], s2.at[k], r2.at[k], (to_y if k % 2 == 0 else to_x, z)
-        )
-        c.start()
-        second.append(c)
-
-    def send_third(k):
-        second[k].wait_recv()
-
-        def add_in(j, carry):
-            came = recv1[k, y, j] if k % 2 == 0 else recv1[k, x, j]
-            value = part[k, y, x, j].astype(jnp.float32) + came.astype(jnp.float32)
-            value = value + recv2[k, j].astype(jnp.float32)
-            plane[k, j] = value.astype(plane.dtype)
-            return carry
-
-        lax.fori_loop(0, members, add_in, 0)
-        if steps[k]:
-            c = remote(
-                plane.at[k], zrecv.at[k], s3.at[k], r3.at[k],
-                (me, lax.rem(z + steps[k], n_shard)),
-            )
-            c.start()
-            third.append(c)
-
-    launch(0)
-    send_first(0)
-    launch(1)
-    send_first(1)
-    for k in range(2, n_shard):
-        launch(k)
-    for k in range(0, n_shard, 2):
-        pair = [i for i in (k, k + 1) if i < n_shard]
-        for i in pair:
-            send_second(i)
-        for i in (k + 2, k + 3):
-            if i < n_shard:
-                send_first(i)
-        for i in pair:
-            send_third(i)
-    for c in third:
-        c.wait_recv()
-
-    def add_last(j, carry):
-        value = plane[n_shard - 1, j].astype(jnp.float32)
-        for k in range(n_shard - 1):
-            value = value + zrecv[k, j].astype(jnp.float32)
-        value = (value * inverse).astype(gown_ref.dtype)
-        gown_ref[j] = value
-        value = value.astype(jnp.float32)
-        line = jnp.sum(value * value, axis=0, keepdims=True)
-        lanes = sq_ref.shape[-1]
-        fold = line[:, :lanes]
-        for i in range(1, cols // lanes):
-            fold = fold + line[:, i * lanes : (i + 1) * lanes]
-        sq_ref[j] = fold
-        return carry
-
-    lax.fori_loop(0, members, add_last, 0)
-    for c in first + second + third:
-        c.wait_send()
+        lax.fori_loop(0, members, add_last, 0)
+
+    def leave():
+        for key in order:
+            swap[key].wait_send()
+            hop[key].wait_send()
+            onward[key].wait_send()
+        for pair in sums + lines:
+            for c in pair:
+                c.wait_send()
+
+    return enter, begin, run, leave
 
 
 HOMES = ((1, 0), (2, 0), (2, 1))
@@ -401,10 +457,11 @@
     return root_scr[...] * (inverse * scale)
 
 
-def settle_kernel(
-    n_shard, scale, owner_ref, start_ref, momentum_hbm, gown_ref, sq_ref,
+def muon_kernel(
+    n_shard, inverse, scale, owner_ref, start_ref, act_ref, cot_ref, momentum_hbm,
     mout_ref, u_ref, wall_ref, qall_ref,
     momentum, gall, sqall, table, factor, uown, held, gram_out, gram_in, gram_scr, root_scr, root,
+    act, cot, turned, part, recv, plane, far, zrecv, reduce_sems,
     load, ps, pr, qs, qr, gs, gr, as_, ar, ws, wr, os_, or_, rs, rr, hs, hr,
 ):
     f32, bf16 = jnp.float32, jnp.bfloat16
@@ -412,24 +469,31 @@
     z = lax.axis_index("shard")
     base = me - core
     block = lax.div(me, 2)
-    members, rows, cols = gown_ref.shape
-    lanes = sq_ref.shape[-1]
+    members = gall.shape[1]
+    rows, cols = held.shape[1:]
+    lanes = sqall.shape[-1]
     other = 1 - 2 * core
     near = (to_core, to_x, to_y, to_xy, to_x + other, to_y + other, to_xy + other)
     mine = pl.ds(pl.multiple_of(core * rows, rows), rows)
 
     fetch = pltpu.make_async_copy(momentum_hbm, momentum, load)
-    fetch.start()
+    enter, begin, run, leave = gather_reduce(
+        n_shard, inverse, act_ref, cot_ref, gall, sqall, act, cot, turned, part, recv,
+        plane, far, zrecv, *reduce_sems,
+    )
+    enter()
     column = [(base + c, lax.rem(z + d, n_shard)) for d in range(1, n_shard) for c in range(2)]
     greet([(p, z) for p in near] + column)
 
-    sqall[0, me] = sq_ref[...]
+    begin()
+    fetch.start()
+    run()
+
     squares = []
     for k, peer in enumerate(near):
         c = remote(sqall.at[0, me], sqall.at[0, me], ps.at[k], pr.at[k], (peer, z))
         c.start()
         squares.append(c)
-    gall[block, :, mine] = gown_ref[...]
     at_g = block_at(gall, 2, rows)
     gathers = plane_gather_start(z, at_g, gs, gr)
     for c in squares:
@@ -626,6 +690,7 @@
         c.wait_send()
     for c in squares + lines:
         c.wait_send()
+    leave()
 
 
 def finish_kernel(
@@ -701,40 +766,18 @@
         return pltpu.CompilerParams(vmem_limit_bytes=limit * 1024 * 1024, **rest)
 
     dma = pltpu.SemaphoreType.DMA
-    gown, sq = pl.pallas_call(
-        functools.partial(reduce_kernel, n_shard, 1.0 / math.sqrt(token_total)),
-        out_shape=(
-            pltpu.VMEM((members, rows, cols), bf16),
-            pltpu.VMEM((members, 1, lanes), f32),
-        ),
-        in_specs=[ANY_SPEC, ANY_SPEC],
-        out_specs=(VMEM_SPEC, VMEM_SPEC),
-        scratch_shapes=[
-            [pltpu.VMEM((layers, 2 * tok_rows, cols), bf16) for _ in range(n_shard)],
-            pltpu.VMEM((layers, 2 * tok_rows, 2 * KV), bf16),
-            pltpu.VMEM((n_shard, 2, 2, members, rows, cols), bf16),
-            pltpu.VMEM((n_shard, 2, members, rows, cols), bf16),
-            pltpu.VMEM((n_shard, members, rows, cols), bf16),
-            pltpu.VMEM((n_shard, members, rows, cols), bf16),
-            pltpu.VMEM((n_shard, members, rows, cols), bf16),
-            pltpu.VMEM((n_shard - 1, members, rows, cols), bf16),
-            dma((n_shard + 1,)), dma((n_shard + 1,)), dma((n_shard + 1,)),
-            dma((n_shard,)), dma((n_shard,)), dma((n_shard,)), dma((n_shard,)),
-            dma((n_shard,)), dma((n_shard,)),
-        ],
-        compiler_params=params(44, has_side_effects=True, collective_id=0),
-        name="reduce",
-    )(activations, cotangents)
-
+    tokens = 4 * tok_rows
+    shares = (layers // 3, layers // 6)
+    hbm = functools.partial(pltpu.with_memory_space_constraint, memory_space=pltpu.HBM)
     mout, turned, wall, qall = pl.pallas_call(
-        functools.partial(settle_kernel, n_shard, update_scale),
+        functools.partial(muon_kernel, n_shard, 1.0 / math.sqrt(token_total), update_scale),
         out_shape=(
             pltpu.VMEM((MATS, KV, cols), f32),
             pltpu.VMEM((MATS, KV, cols), bf16),
             pltpu.VMEM((n_shard - 1, slots, KV, cols), bf16),
             pltpu.VMEM((groups, members, KV, KV), bf16),
         ),
-        in_specs=[SMEM_SPEC, SMEM_SPEC, ANY_SPEC, VMEM_SPEC, VMEM_SPEC],
+        in_specs=[SMEM_SPEC, SMEM_SPEC, ANY_SPEC, ANY_SPEC, ANY_SPEC],
         out_specs=(VMEM_SPEC,) * 4,
         scratch_shapes=[
             pltpu.VMEM((MATS, KV, cols), f32),
@@ -749,6 +792,17 @@
             pltpu.VMEM((KV, KV), f32),
             pltpu.VMEM((KV, KV), f32),
             pltpu.VMEM((KV, KV), bf16),
+            [pltpu.VMEM((n_shard, n, tokens, cols), bf16) for n in shares],
+            [pltpu.VMEM((n, tokens, 2 * KV), bf16) for n in shares],
+            [pltpu.VMEM((n, 2, rows, tokens), bf16) for n in shares],
+            [pltpu.VMEM((n_shard, 2, n, rows, cols), bf16) for n in shares],
+            [pltpu.VMEM((n_shard, n, rows, cols), bf16) for n in shares],
+            pltpu.VMEM((n_shard, members, rows, cols), bf16),
+            pltpu.VMEM((members, rows, cols), bf16),
+            pltpu.VMEM((n_shard - 1, members, rows, cols), bf16),
+            [dma((2, n_shard + 1)) for _ in range(7)]
+            + [dma((2, n_shard)) for _ in range(2)]
+            + [dma((n_shard - 1, 2)) for _ in range(2)],
             dma(()),
             dma((7,)), dma((7,)), dma((n_shard - 1,)), dma((n_shard - 1,)),
             dma((10,)), dma((10,)),
@@ -758,9 +812,9 @@
             dma((2 * n_shard - 1,)), dma((members,)),
             dma((10,)), dma((10,)),
         ],
-        compiler_params=params(32, has_side_effects=True, collective_id=1),
-        name="settle",
-    )(owners, bucket_starts, momentum, gown, sq)
+        compiler_params=params(48, has_side_effects=True, collective_id=0),
+        name="muon",
+    )(owners, bucket_starts, hbm(activations), hbm(cotangents), hbm(momentum))
 
     return pl.pallas_call(
         finish_kernel,

time: 145 us -> 113 us (0.78)
  Pallas kernels: 137 us -> 112 us
  local copies, waits for them, and re-layouts: 7.1 us -> 0.01 us
    pallas_call x2 -> x1, Pallas kernels: 130 us -> 106 us  [per_device_planes(): pl.pallas_call(functools.partial(muon_kernel, n_shard, 1.0 / math.sqrt(to...]
    unnamed x10 -> x2, local copies, waits for them, and re-layouts: 7.1 us -> 0.01 us
where the time goes in v2:
time: 113 us
  Pallas kernels  112 us (99%)
    pallas_call x1, Pallas kernels, per_device_planes(): pl.pallas_call(functools.partial(muon_kernel, n_shard, 1.0 / math.sqrt(to...  106 us
    pallas_call x1, Pallas kernels, per_device_planes(): pl.pallas_call(finish_kernel, out_shape=(jax.ShapeDtypeStruct(momentum.sh...  6.57 us

profile of v2, /device:TPU:0, one launch (start us, length us, event | category | flops | bytes accessed | tf_op | source)
XLA Modules:
  0.0 113.1 jit_solution(5315271364465781931)
XLA Ops:
  0.6 0.0 copy-start
  0.6 105.9 %muon.1 = (f32[12,256,512]{2,1,0:T(8,128)S(1)}, bf16[12,256,512]{2,1,0:T(8,128)(2,1)S(1)}, bf16[3,4,256,512]{3,2,1,0:T(8,128)(2,1)S(1)}, bf16[4,3,256,256]{3,2,1,0:T(8,128)(2,1)S(1)}) custom-call(s32[12]{0:T(128)} %owner_ref.3, s32[2]{0:T(128)} %start_ref.1, bf16[6,128,2048]{2,1,0:T(8,128)(2,1)} %act_ref.1, bf16[6,128,512]{2,1,0:T(8,128)(2,1)} %cot_ref.1, ...), custom_call_target="tpu_custom_call" | custom-call | tf_op jit(solution)/shard_map/muon/pallas_call | solution.py:772
  106.6 0.0 copy-done
  106.6 6.6 %finish.1 = (f32[12,256,512]{2,1,0:T(8,128)}, f32[12,256,512]{2,1,0:T(8,128)}, bf16[4,256,2048]{2,1,0:T(8,128)(2,1)}) custom-call(s32[12]{0:T(128)S(1)} %copy-done, f32[12,256,512]{2,1,0:T(8,128)S(1)} %get-tuple-element.7.mout_ref, bf16[12,256,512]{2,1,0:T(8,128)(2,1)S(1)} %get-tuple-element.8.u_ref, bf16[3,4,256,512]{3,2,1,0:T(8,128)(2,1)S(1)} %get-tuple-element.9.wall_ref, ...), custom_call_target="tpu_custom_call" | custom-call | tf_op jit(solution)/shard_map/finish/pallas_call | solution.py:819
Async XLA Ops:
  0.6 105.9 %copy-start = (s32[12]{0:T(128)S(1)}, s32[12]{0:T(128)}, u32[]{:S(2)}) copy-start(s32[12]{0:T(128)} %owner_ref.3) | copy-start | bytes 148

commit v3 on v2

--- a/solution.py
+++ b/solution.py
@@ -164,7 +164,7 @@
     plan = ((0, to_x, 0), (2, to_y, 1), (1, to_x, 1), (3, to_y, 0), (4, to_core, None))
     copies = {}
     for k, peer, half in plan:
-        copies[k] = remote(at(me, half), at(me, half), send.at[k], recv.at[k], (peer, z))
+        copies[k] = remote(at(me, half), at(me, half), send, recv.at[k], (peer, z))
         copies[k].start()
     return copies
 
@@ -174,7 +174,7 @@
 
     def forward(k, block, half, peer):
         copies[k] = remote(
-            at(block, half), at(block, half), send.at[k], recv.at[k], (peer, z)
+            at(block, half), at(block, half), send, recv.at[k], (peer, z)
         )
         copies[k].start()
 
@@ -193,18 +193,20 @@
     copies[5].wait_recv()
     copies[6].wait_recv()
     copies[9] = remote(
-        at(to_xy, None), at(to_xy, None), send.at[9], recv.at[9], (to_core, z)
+        at(to_xy, None), at(to_xy, None), send, recv.at[9], (to_core, z)
     )
     copies[9].start()
     for k in last:
         copies[k].wait_recv()
-    for k in range(10):
-        copies[k].wait_send()
+
+
+def drain(ref, semaphore):
+    pltpu.make_async_copy(ref, ref, semaphore).wait()
 
 
 def gather_reduce(
     n_shard, inverse, act_ref, cot_ref, gall, sqall, act, cot, turned, part, recv, plane, far, zrecv,
-    own_sem, swap_s, swap_r, hop_s, hop_r, pass_s, pass_r, sum_s, sum_r, line_s, line_r,
+    in_sem, hop_r, swap_s, hop_s, pass_s, sum_s, sum_r, line_s, line_r,
 ):
     f32 = jnp.float32
     me, core, x, y, to_core, to_x, to_y, to_xy = place()
@@ -220,53 +222,42 @@
     mine = (counts[0] * x, shared + counts[1] * y)
     yours = (counts[0] * (1 - x), shared + counts[1] * (1 - y))
     peers = (to_x, to_y)
-    waits = []
+    layer_of = ((1 - y, y), (0,))
+    keys = [(1, n_shard, 0), (0, n_shard, 0), (1, 0, 0), (0, 0, 0), (0, n_shard, 1), (0, 0, 1)]
+    keys += [(kind, k, j) for k in range(1, n_shard) for kind, j in ((1, 0), (0, 0), (0, 1))]
+
+    def index(kind, k, j):
+        return 2 * k + j if kind == 0 else 2 * (n_shard + 1) + k
 
     def source(kind, k, layer):
-        span = pl.ds(layer, counts[kind])
-        return cot_ref.at[span] if k == n_shard else act_ref.at[span, :, cut[k]]
-
-    def slot(kind, k, s):
-        buffer = cot[kind] if k == n_shard else act[kind].at[k]
-        return buffer.at[:, pl.ds(s * tokens, tokens)]
-
-    order = [(1, n_shard), (0, n_shard)] + [(kind, k) for k in range(n_shard) for kind in (1, 0)]
-    own = {
-        (kind, k): pltpu.make_async_copy(
-            source(kind, k, mine[kind]), slot(kind, k, 0), own_sem.at[kind, k]
+        return cot_ref.at[layer] if k == n_shard else act_ref.at[layer, :, cut[k]]
+
+    def slots(kind, k, j, first, count):
+        layer = layer_of[kind][j]
+        buffer = cot[kind].at[layer] if k == n_shard else act[kind].at[k, layer]
+        return buffer.at[pl.ds(first * tokens, count * tokens)]
+
+    own, swap, hop, onward = {}, {}, {}, {}
+    for key in keys:
+        kind, k, j = key
+        at = in_sem.at[index(*key)]
+        group = 2 * kind + (1 if k == n_shard else 0)
+        layer = layer_of[kind][j]
+        here = source(kind, k, mine[kind] + layer)
+        own[key] = pltpu.make_async_copy(here, slots(*key, 0, 1), at)
+        swap[key] = remote(here, slots(*key, 1, 1), swap_s.at[group], at, (to_core, z))
+        hop[key] = remote(
+            source(kind, k, yours[kind] + layer), slots(*key, 3, 1),
+            hop_s.at[group], hop_r.at[index(*key)], (peers[kind], z),
         )
-        for kind, k in order
-    }
-    swap = {
-        (kind, k): remote(
-            source(kind, k, mine[kind]), slot(kind, k, 1),
-            swap_s.at[kind, k], swap_r.at[kind, k], (to_core, z),
-        )
-        for kind, k in order
-    }
-    hop = {
-        (kind, k): remote(
-            source(kind, k, yours[kind]), slot(kind, k, 2),
-            hop_s.at[kind, k], hop_r.at[kind, k], (peers[kind], z),
-        )
-        for kind, k in order
-    }
-    onward = {
-        (kind, k): remote(
-            slot(kind, k, 2), slot(kind, k, 3),
-            pass_s.at[kind, k], pass_r.at[kind, k], (to_core, z),
-        )
-        for kind, k in order
-    }
+        onward[key] = remote(slots(*key, 3, 1), slots(*key, 2, 1), pass_s.at[group], at, (to_core, z))
     sums = [
         [
             remote(
-                part[0].at[k, 1 - y], recv[0].at[k],
-                sum_s.at[0, k], sum_r.at[0, k], (to_y, z),
+                part[0].at[k, 1 - y], recv[0].at[k], sum_s.at[0], sum_r.at[0, k], (to_y, z)
             ),
             remote(
-                part[1].at[k, 1 - x], recv[1].at[k],
-                sum_s.at[1, k], sum_r.at[1, k], (to_x, z),
+                part[1].at[k, 1 - x], recv[1].at[k], sum_s.at[1], sum_r.at[1, k], (to_x, z)
             ),
         ]
         for k in range(n_shard)
@@ -276,7 +267,7 @@
         [
             remote(
                 (far if m == 1 else plane.at[m]).at[spans[kind]], zrecv.at[m, spans[kind]],
-                line_s.at[m, kind], line_r.at[m, kind], (me, across if m == 1 else near),
+                line_s.at[kind], line_r.at[m, kind], (me, across if m == 1 else near),
             )
             for kind in range(2)
         ]
@@ -284,38 +275,40 @@
     ]
 
     def enter():
-        for key in order:
+        for key in keys:
             own[key].start()
 
+    def send(kind, k):
+        for j in range(counts[kind]):
+            hop[kind, k, j].start()
+
     def begin():
-        for key in order:
-            if key != (0, n_shard - 1):
-                hop[key].start()
-        for key in order:
+        for key in keys[:6]:
+            hop[key].start()
+        send(1, 1)
+        send(0, 1)
+        for key in keys:
             swap[key].start()
 
-    def take(kind, k):
-        hop[kind, k].wait_recv()
-        onward[kind, k].start()
-
-    def ready(kind, k):
-        own[kind, k].wait()
-        swap[kind, k].wait_recv()
-        onward[kind, k].wait_recv()
-
-    def turn(kind):
-        ready(kind, n_shard)
-        for layer in range(counts[kind]):
-            for side in range(2):
-                at = pl.ds(pl.multiple_of((2 * side + core) * rows, rows), rows)
-                turned[kind][layer, side] = cot[kind][layer, :, at].T
-
-    def product(kind, k):
-        ready(kind, k)
-
-        def one(q, carry):
-            layer = lax.div(q, 2)
-            side = lax.rem(q, 2)
+    def take(kind, k, j=0):
+        hop[kind, k, j].wait_recv()
+        onward[kind, k, j].start()
+
+    def ready(kind, k, j):
+        drain(slots(kind, k, j, 0, 3), in_sem.at[index(kind, k, j)])
+
+    def turn(kind, j=0):
+        ready(kind, n_shard, j)
+        layer = layer_of[kind][j]
+        for side in range(2):
+            at = pl.ds(pl.multiple_of((2 * side + core) * rows, rows), rows)
+            turned[kind][layer, side] = cot[kind][layer, :, at].T
+
+    def product(kind, k, j=0):
+        ready(kind, k, j)
+        layer = layer_of[kind][j]
+
+        def one(side, carry):
             value = jnp.dot(turned[kind][layer, side], act[kind][k, layer], preferred_element_type=f32)
             if kind == 0:
                 part[0][k, layer, side] = value.astype(part[0].dtype)
@@ -323,8 +316,9 @@
                 part[1][k, side, 0] = value.astype(part[1].dtype)
             return carry
 
-        lax.fori_loop(0, 2 * counts[kind], one, 0)
-        sums[k][kind].start()
+        lax.fori_loop(0, 2, one, 0)
+        if j == 0:
+            sums[k][kind].start()
 
     def gather(kind, k):
         sums[k][kind].wait_recv()
@@ -342,38 +336,51 @@
 
     def run():
         take(1, n_shard)
+        take(0, n_shard, 0)
+        turn(1)
         take(1, 0)
-        take(0, n_shard)
-        turn(1)
+        take(0, 0, 0)
+        turn(0, 0)
         product(1, 0)
+        product(0, 0, 0)
+        send(1, 2)
         take(1, 1)
-        turn(0)
+        take(0, n_shard, 1)
         product(1, 1)
-        hop[0, n_shard - 1].start()
-        take(0, 0)
-        take(1, 2)
-        product(0, 0)
-        product(1, 2)
-        take(1, 3)
-        product(1, 3)
-        take(0, 1)
-        product(0, 1)
+        send(0, 2)
+        turn(0, 1)
+        take(0, 0, 1)
+        product(0, 0, 1)
+        take(0, 1, 0)
+        product(0, 1, 0)
+        send(1, 3)
         gather(0, 0)
         lines[0][0].start()
-        take(0, 2)
-        product(0, 2)
+        take(0, 1, 1)
+        product(0, 1, 1)
+        take(1, 2)
+        product(1, 2)
+        send(0, 3)
         gather(1, 0)
         lines[0][1].start()
         gather(0, 1)
         gather(1, 1)
         cross(0)
+        take(0, 2, 0)
+        product(0, 2, 0)
         cross(1)
+        take(1, 3)
+        product(1, 3)
+        take(0, 2, 1)
+        product(0, 2, 1)
+        gather(1, 2)
+        lines[2][1].start()
         gather(0, 2)
         lines[2][0].start()
-        take(0, 3)
-        product(0, 3)
-        gather(1, 2)
-        lines[2][1].start()
+        take(0, 3, 0)
+        product(0, 3, 0)
+        take(0, 3, 1)
+        product(0, 3, 1)
         gather(1, 3)
         gather(0, 3)
         for m in (2, 1):
@@ -394,19 +401,18 @@
             fold = line[:, :lanes]
             for i in range(1, cols // lanes):
                 fold = fold + line[:, i * lanes : (i + 1) * lanes]
-            sqall[0, me, j] = fold
+            sqall[me * n_shard + z, j] = fold
             return carry
 
         lax.fori_loop(0, members, add_last, 0)
 
     def leave():
-        for key in order:
-            swap[key].wait_send()
-            hop[key].wait_send()
-            onward[key].wait_send()
-        for pair in sums + lines:
-            for c in pair:
-                c.wait_send()
+        for kind in range(2):
+            for pool in (swap_s, hop_s, pass_s):
+                drain(act[kind].at[:, :, pl.ds(0, tokens)], pool.at[2 * kind])
+                drain(cot[kind].at[:, pl.ds(0, tokens)], pool.at[2 * kind + 1])
+            drain(recv[kind], sum_s.at[kind])
+            drain(zrecv.at[:, spans[kind]], line_s.at[kind])
 
     return enter, begin, run, leave
 
@@ -462,7 +468,7 @@
     mout_ref, u_ref, wall_ref, qall_ref,
     momentum, gall, sqall, table, factor, uown, held, gram_out, gram_in, gram_scr, root_scr, root,
     act, cot, turned, part, recv, plane, far, zrecv, reduce_sems,
-    load, ps, pr, qs, qr, gs, gr, as_, ar, ws, wr, os_, or_, rs, rr, hs, hr,
+    load, ps, pr, gs, gr, as_, ar, ws, wr, os_, or_, rs, rr, hs, hr,
 ):
     f32, bf16 = jnp.float32, jnp.bfloat16
     me, core, x, y, to_core, to_x, to_y, to_xy = place()
@@ -472,8 +478,6 @@
     members = gall.shape[1]
     rows, cols = held.shape[1:]
     lanes = sqall.shape[-1]
-    other = 1 - 2 * core
-    near = (to_core, to_x, to_y, to_xy, to_x + other, to_y + other, to_xy + other)
     mine = pl.ds(pl.multiple_of(core * rows, rows), rows)
 
     fetch = pltpu.make_async_copy(momentum_hbm, momentum, load)
@@ -482,39 +486,31 @@
         plane, far, zrecv, *reduce_sems,
     )
     enter()
-    column = [(base + c, lax.rem(z + d, n_shard)) for d in range(1, n_shard) for c in range(2)]
-    greet([(p, z) for p in near] + column)
+    everyone = n_shard * 2 * gall.shape[0]
+    here = me * n_shard + z
+    others = [lax.rem(here + t, everyone) for t in range(1, everyone)]
+    others = [(lax.div(to, n_shard), lax.rem(to, n_shard)) for to in others]
+    greet(others)
 
     begin()
     fetch.start()
     run()
 
-    squares = []
-    for k, peer in enumerate(near):
-        c = remote(sqall.at[0, me], sqall.at[0, me], ps.at[k], pr.at[k], (peer, z))
-        c.start()
-        squares.append(c)
+    for peer in others:
+        remote(sqall.at[here], sqall.at[here], ps, pr, peer).start()
     at_g = block_at(gall, 2, rows)
     gathers = plane_gather_start(z, at_g, gs, gr)
-    for c in squares:
-        c.wait_recv()
-    lines = []
-    for d in range(1, n_shard):
-        c = remote(sqall.at[0], sqall.at[d], qs.at[d - 1], qr.at[d - 1], (me, lax.rem(z + d, n_shard)))
-        c.start()
-        lines.append(c)
     fetch.wait()
-    for c in lines:
-        c.wait_recv()
+    drain(sqall.at[pl.ds(0, everyone - 1)], pr)
 
     table[...] = jnp.zeros_like(table)
     for m in range(MATS):
         layer, side = divmod(m, 2)
         bx, by = divmod(layer, 2) if m < 8 else (side, layer - 4)
         j, i = 2 * by + bx, side if m < 8 else 2
-        line = sqall[0, 2 * j, i] + sqall[0, 2 * j + 1, i]
-        for d in range(1, n_shard):
-            line = line + sqall[d, 2 * j, i] + sqall[d, 2 * j + 1, i]
+        line = sqall[2 * j * n_shard, i]
+        for d in range(1, 2 * n_shard):
+            line = line + sqall[2 * j * n_shard + d, i]
         table[pl.ds(m, 1)] = line
     index = lax.broadcasted_iota(jnp.int32, table.shape, 0)
     bucket = jnp.zeros(table.shape, jnp.int32)
@@ -588,18 +584,20 @@
             count = count + yes.astype(jnp.int32)
         return found
 
-    sends = []
-    for d in (1, 3, 2):
+    sends = {}
+
+    def send_slice(d):
         shard = lax.rem(z + d, n_shard)
         matrix = slot_matrix(shard, block)
         home, member = lodging(matrix)
         held[d - 1] = advance(matrix, gall[home, member, mine], momentum[matrix, mine])[1]
-        c = remote(
-            held.at[d - 1], wall_ref.at[n_shard - d - 1, block, mine],
-            ws.at[d - 1], wr.at[d - 1], (me, shard),
+        sends[d] = remote(
+            held.at[d - 1], wall_ref.at[n_shard - d - 1, block, mine], ws, wr.at[d - 1], (me, shard)
         )
-        c.start()
-        sends.append((d, c))
+        sends[d].start()
+
+    send_slice(1)
+    send_slice(3)
 
     def all_one(m, carry):
         home, member = lodging(m)
@@ -607,8 +605,6 @@
         mout_ref[m] = new
         u_ref[m] = turned
         return carry
-
-    lax.fori_loop(0, MATS, all_one, 0)
 
     is_home = functools.reduce(jnp.logical_or, [here for here, _, _ in parts])
     member = jnp.where(z == HOMES[0][0], 0, 1 + core)
@@ -620,8 +616,7 @@
             peer = (to_core, z) if d == 0 else (base + c, lax.rem(z + d, n_shard))
             half = 1 - core if d == 0 else c
             cut = pl.ds(pl.multiple_of(half * rows, rows), rows)
-            k = len(roots)
-            roots.append(remote(root.at[cut], qall_ref.at[block, member, cut], rs.at[k], rr.at[member], peer))
+            roots.append(remote(root.at[cut], qall_ref.at[block, member, cut], rs, rr.at[member], peer))
 
     @pl.when(is_home)
     def _():
@@ -648,15 +643,20 @@
             c.start()
         qall_ref[block, member, mine] = root[mine]
 
-    at_w = {d: block_at(wall_ref.at[n_shard - d - 1], 1, rows) for d, _ in sends}
     walls = {}
-    for d, c in sends:
-        c.wait_recv()
-        walls[d] = plane_gather_start(z, at_w[d], os_.at[d - 1], or_.at[d - 1])
-    order = [d for d, _ in sends]
-    plane_gather_turn(z, at_w[order[0]], os_.at[order[0] - 1], or_.at[order[0] - 1], walls[order[0]])
+
+    def at_w(d):
+        return block_at(wall_ref.at[n_shard - d - 1], 1, rows)
+
+    for d in (1, 3):
+        sends[d].wait_recv()
+        walls[d] = plane_gather_start(z, at_w(d), os_.at[d - 1], or_.at[d - 1])
+    send_slice(2)
+    lax.fori_loop(0, MATS, all_one, 0)
+    for d in (1, 3):
+        plane_gather_turn(z, at_w(d), os_.at[d - 1], or_.at[d - 1], walls[d])
     for i, (here, _, _) in enumerate(parts):
-        arrival = remote(root.at[mine], qall_ref.at[block, i, mine], rs.at[0], rr.at[i], (to_core, z))
+        arrival = remote(root.at[mine], qall_ref.at[block, i, mine], rs, rr.at[i], (to_core, z))
 
         @pl.when(jnp.logical_not(here))
         def _():
@@ -664,17 +664,25 @@
 
     at_q = block_at(qall_ref, 2, rows)
     gathers_q = plane_gather_start(z, at_q, hs, hr)
-    for d in order[1:]:
-        plane_gather_turn(z, at_w[d], os_.at[d - 1], or_.at[d - 1], walls[d])
+    sends[2].wait_recv()
+    walls[2] = plane_gather_start(z, at_w(2), os_.at[1], or_.at[1])
+    for d in (1, 3):
+        plane_gather_finish(z, at_w(d), os_.at[d - 1], or_.at[d - 1], walls[d])
     plane_gather_turn(z, at_q, hs, hr, gathers_q)
-    for d in order:
-        plane_gather_finish(z, at_w[d], os_.at[d - 1], or_.at[d - 1], walls[d])
+    plane_gather_turn(z, at_w(2), os_.at[1], or_.at[1], walls[2])
     plane_gather_finish(z, at_q, hs, hr, gathers_q)
+    plane_gather_finish(z, at_w(2), os_.at[1], or_.at[1], walls[2])
+    most = pl.ds(0, 2 * rows - rows // 4)
+    drain(gall.at[:, :, most], gs)
+    drain(qall_ref.at[:, :, most], hs)
+    for d in range(n_shard - 1):
+        drain(wall_ref.at[d, :, most], os_.at[d])
+    drain(held, ws)
+    drain(sqall.at[pl.ds(0, everyone - 1)], ps)
 
     @pl.when(is_home)
     def _():
-        for c in roots:
-            c.wait_send()
+        drain(u_ref.at[pl.ds(0, len(roots)), pl.ds(0, rows // 2)], rs)
 
     for here, part, cross in parts:
 
@@ -686,10 +694,6 @@
             def _():
                 cross.wait_send()
 
-    for _, c in sends:
-        c.wait_send()
-    for c in squares + lines:
-        c.wait_send()
     leave()
 
 
@@ -782,7 +786,7 @@
         scratch_shapes=[
             pltpu.VMEM((MATS, KV, cols), f32),
             pltpu.VMEM((groups, members, KV, cols), bf16),
-            pltpu.VMEM((n_shard, n_rep, members, 1, lanes), f32),
+            pltpu.VMEM((n_rep * n_shard, members, 1, lanes), f32),
             pltpu.VMEM((16, lanes), f32),
             pltpu.VMEM((MATS, 1, cols), f32),
             pltpu.VMEM((members, KV, cols), bf16),
@@ -800,17 +804,17 @@
             pltpu.VMEM((n_shard, members, rows, cols), bf16),
             pltpu.VMEM((members, rows, cols), bf16),
             pltpu.VMEM((n_shard - 1, members, rows, cols), bf16),
-            [dma((2, n_shard + 1)) for _ in range(7)]
-            + [dma((2, n_shard)) for _ in range(2)]
-            + [dma((n_shard - 1, 2)) for _ in range(2)],
+            [dma((3 * n_shard + 3,)) for _ in range(2)]
+            + [dma((4,)) for _ in range(3)]
+            + [dma((2,)), dma((2, n_shard)), dma((2,)), dma((n_shard - 1, 2))],
             dma(()),
-            dma((7,)), dma((7,)), dma((n_shard - 1,)), dma((n_shard - 1,)),
-            dma((10,)), dma((10,)),
+            dma(()), dma(()),
+            dma(()), dma((10,)),
             dma((members, 2)), dma((n_shard, 3)),
-            dma((n_shard - 1,)), dma((n_shard - 1,)),
-            dma((n_shard - 1, 10)), dma((n_shard - 1, 10)),
-            dma((2 * n_shard - 1,)), dma((members,)),
-            dma((10,)), dma((10,)),
+            dma(()), dma((n_shard - 1,)),
+            dma((n_shard - 1,)), dma((n_shard - 1, 10)),
+            dma(()), dma((members,)),
+            dma(()), dma((10,)),
         ],
         compiler_params=params(48, has_side_effects=True, collective_id=0),
         name="muon",

time: 113 us -> 113 us (level)
  no operation moved by 1% of the time
where the time goes in v3:
time: 113 us; the launch traced here: 112 us
  Pallas kernels  112 us (99%)
    pallas_call x1, Pallas kernels, per_device_planes(): pl.pallas_call(functools.partial(muon_kernel, n_shard, 1.0 / math.sqrt(to...  105 us
    pallas_call x1, Pallas kernels, per_device_planes(): pl.pallas_call(finish_kernel, out_shape=(jax.ShapeDtypeStruct(momentum.sh...  6.57 us

profile of v3, /device:TPU:0, one launch (start us, length us, event | category | flops | bytes accessed | tf_op | source)
XLA Modules:
  0.0 112.5 jit_solution(5144061712109106745)
XLA Ops:
  0.6 0.0 copy-start
  0.6 105.3 %muon.1 = (f32[12,256,512]{2,1,0:T(8,128)S(1)}, bf16[12,256,512]{2,1,0:T(8,128)(2,1)S(1)}, bf16[3,4,256,512]{3,2,1,0:T(8,128)(2,1)S(1)}, bf16[4,3,256,256]{3,2,1,0:T(8,128)(2,1)S(1)}) custom-call(s32[12]{0:T(128)} %owner_ref.3, s32[2]{0:T(128)} %start_ref.1, bf16[6,128,2048]{2,1,0:T(8,128)(2,1)} %act_ref.1, bf16[6,128,512]{2,1,0:T(8,128)(2,1)} %cot_ref.1, ...), custom_call_target="tpu_custom_call" | custom-call | tf_op jit(solution)/shard_map/muon/pallas_call | solution.py:776
  105.9 0.0 copy-done
  105.9 6.6 %finish.1 = (f32[12,256,512]{2,1,0:T(8,128)}, f32[12,256,512]{2,1,0:T(8,128)}, bf16[4,256,2048]{2,1,0:T(8,128)(2,1)}) custom-call(s32[12]{0:T(128)S(1)} %copy-done, f32[12,256,512]{2,1,0:T(8,128)S(1)} %get-tuple-element.7.mout_ref, bf16[12,256,512]{2,1,0:T(8,128)(2,1)S(1)} %get-tuple-element.8.u_ref, bf16[3,4,256,512]{3,2,1,0:T(8,128)(2,1)S(1)} %get-tuple-element.9.wall_ref, ...), custom_call_target="tpu_custom_call" | custom-call | tf_op jit(solution)/shard_map/finish/pallas_call | solution.py:823
Async XLA Ops:
  0.6 105.3 %copy-start = (s32[12]{0:T(128)S(1)}, s32[12]{0:T(128)}, u32[]{:S(2)}) copy-start(s32[12]{0:T(128)} %owner_ref.3) | copy-start | bytes 148

commit v4 on v3

--- a/solution.py
+++ b/solution.py
@@ -205,7 +205,7 @@
 
 
 def gather_reduce(
-    n_shard, inverse, act_ref, cot_ref, gall, sqall, act, cot, turned, part, recv, plane, far, zrecv,
+    n_shard, inverse, act_ref, cot_ref, gall, sqall, act, cot, turned, part, recv, plane, zrecv,
     in_sem, hop_r, swap_s, hop_s, pass_s, sum_s, sum_r, line_s, line_r,
 ):
     f32 = jnp.float32
@@ -214,8 +214,10 @@
     tokens = act_ref.shape[1]
     members, rows, cols = plane.shape[1:]
     near = z + 1 - 2 * lax.rem(z, 2)
-    across = z + 2 - 4 * lax.div(z, 2)
-    targets = (n_shard - 1 - z, across, near, z)
+    low = z < 2
+    inner = (z == 1) | (z == 2)
+    inward = jnp.where(low, z + 1, z - 1)
+    targets = (jnp.where(low, 3, 0), jnp.where(low, 2, 1), near, z)
     cut = [pl.ds(pl.multiple_of(t * cols, cols), cols) for t in targets]
     counts = [c.shape[0] for c in cot]
     shared = counts[0] * 2
@@ -266,13 +268,22 @@
     lines = [
         [
             remote(
-                (far if m == 1 else plane.at[m]).at[spans[kind]], zrecv.at[m, spans[kind]],
-                line_s.at[kind], line_r.at[m, kind], (me, across if m == 1 else near),
+                plane.at[k, spans[kind]],
+                zrecv.at[k if k == 2 else k + 3 * inner.astype(jnp.int32), spans[kind]],
+                line_s.at[kind],
+                line_r.at[k if k == 2 else k + 3 * inner.astype(jnp.int32), kind],
+                (me, near if k == 2 else inward),
             )
             for kind in range(2)
         ]
-        for m in range(n_shard - 1)
+        for k in range(n_shard - 1)
     ]
+
+    def arrived(s, kind):
+        remote(
+            plane.at[0, spans[kind]], zrecv.at[s, spans[kind]], line_s.at[kind], line_r.at[s, kind],
+            (me, near),
+        ).wait_recv()
 
     def enter():
         for key in keys:
@@ -327,12 +338,21 @@
             value = kept.astype(f32) + recv[kind][k, i].astype(f32)
             plane[k, i if kind == 0 else members - 1] = value.astype(plane.dtype)
 
-    def cross(kind):
-        lines[0][kind].wait_recv()
-        for i in range(members - 1) if kind == 0 else (members - 1,):
-            value = plane[1, i].astype(f32) + zrecv[0, i].astype(f32)
-            far[i] = value.astype(far.dtype)
-        lines[1][kind].start()
+    def release(kind, k):
+        @pl.when(jnp.logical_not(inner))
+        def _():
+            lines[k][kind].start()
+
+    def forward(kind, k):
+        s = 3 if k == 2 else k
+
+        @pl.when(inner)
+        def _():
+            arrived(s, kind)
+            for i in range(members - 1) if kind == 0 else (members - 1,):
+                value = plane[k, i].astype(f32) + zrecv[s, i].astype(f32)
+                plane[k, i] = value.astype(plane.dtype)
+            lines[k][kind].start()
 
     def run():
         take(1, n_shard)
@@ -355,44 +375,49 @@
         product(0, 1, 0)
         send(1, 3)
         gather(0, 0)
-        lines[0][0].start()
+        release(0, 0)
         take(0, 1, 1)
         product(0, 1, 1)
         take(1, 2)
         product(1, 2)
         send(0, 3)
         gather(1, 0)
-        lines[0][1].start()
+        release(1, 0)
         gather(0, 1)
+        release(0, 1)
         gather(1, 1)
-        cross(0)
+        release(1, 1)
+        forward(0, 0)
         take(0, 2, 0)
         product(0, 2, 0)
-        cross(1)
+        forward(1, 0)
         take(1, 3)
         product(1, 3)
         take(0, 2, 1)
         product(0, 2, 1)
+        forward(0, 1)
         gather(1, 2)
-        lines[2][1].start()
+        release(1, 2)
         gather(0, 2)
-        lines[2][0].start()
+        release(0, 2)
+        forward(1, 1)
+        forward(0, 2)
+        forward(1, 2)
         take(0, 3, 0)
         product(0, 3, 0)
         take(0, 3, 1)
         product(0, 3, 1)
         gather(1, 3)
         gather(0, 3)
-        for m in (2, 1):
-            for c in lines[m]:
-                c.wait_recv()
+        for kind in range(2):
+            arrived(2, kind)
         home = lax.div(me, 2)
         half = pl.ds(pl.multiple_of(core * rows, rows), rows)
 
-        def add_last(j, carry):
+        def add_last(others, j):
             value = plane[n_shard - 1, j].astype(f32)
-            for m in (1, 2):
-                value = value + zrecv[m, j].astype(f32)
+            for s in others:
+                value = value + zrecv[s, j].astype(f32)
             value = (value * inverse).astype(gall.dtype)
             gall[home, j, half] = value
             value = value.astype(f32)
@@ -402,9 +427,18 @@
             for i in range(1, cols // lanes):
                 fold = fold + line[:, i * lanes : (i + 1) * lanes]
             sqall[me * n_shard + z, j] = fold
-            return carry
-
-        lax.fori_loop(0, members, add_last, 0)
+
+        @pl.when(inner)
+        def _():
+            for kind in range(2):
+                arrived(4, kind)
+            for j in range(members):
+                add_last((2, 4), j)
+
+        @pl.when(jnp.logical_not(inner))
+        def _():
+            for j in range(members):
+                add_last((2,), j)
 
     def leave():
         for kind in range(2):
@@ -412,7 +446,7 @@
                 drain(act[kind].at[:, :, pl.ds(0, tokens)], pool.at[2 * kind])
                 drain(cot[kind].at[:, pl.ds(0, tokens)], pool.at[2 * kind + 1])
             drain(recv[kind], sum_s.at[kind])
-            drain(zrecv.at[:, spans[kind]], line_s.at[kind])
+            drain(plane.at[pl.ds(0, n_shard - 1), spans[kind]], line_s.at[kind])
 
     return enter, begin, run, leave
 
@@ -467,7 +501,7 @@
     n_shard, inverse, scale, owner_ref, start_ref, act_ref, cot_ref, momentum_hbm,
     mout_ref, u_ref, wall_ref, qall_ref,
     momentum, gall, sqall, table, factor, uown, held, gram_out, gram_in, gram_scr, root_scr, root,
-    act, cot, turned, part, recv, plane, far, zrecv, reduce_sems,
+    act, cot, turned, part, recv, plane, zrecv, reduce_sems,
     load, ps, pr, gs, gr, as_, ar, ws, wr, os_, or_, rs, rr, hs, hr,
 ):
     f32, bf16 = jnp.float32, jnp.bfloat16
@@ -483,7 +517,7 @@
     fetch = pltpu.make_async_copy(momentum_hbm, momentum, load)
     enter, begin, run, leave = gather_reduce(
         n_shard, inverse, act_ref, cot_ref, gall, sqall, act, cot, turned, part, recv,
-        plane, far, zrecv, *reduce_sems,
+        plane, zrecv, *reduce_sems,
     )
     enter()
     everyone = n_shard * 2 * gall.shape[0]
@@ -609,13 +643,15 @@
     is_home = functools.reduce(jnp.logical_or, [here for here, _, _ in parts])
     member = jnp.where(z == HOMES[0][0], 0, 1 + core)
     roots = []
+    packed = root.shape[0] // 2
+    mine_q = pl.ds(pl.multiple_of(core * packed, packed), packed)
     for d in range(n_shard):
         for c in range(2):
             if d == 0 and c == 1:
                 continue
             peer = (to_core, z) if d == 0 else (base + c, lax.rem(z + d, n_shard))
             half = 1 - core if d == 0 else c
-            cut = pl.ds(pl.multiple_of(half * rows, rows), rows)
+            cut = pl.ds(pl.multiple_of(half * packed, packed), packed)
             roots.append(remote(root.at[cut], qall_ref.at[block, member, cut], rs, rr.at[member], peer))
 
     @pl.when(is_home)
@@ -638,10 +674,14 @@
         top = jnp.concatenate([blocks[0], blocks[2]], axis=1)
         bottom = jnp.concatenate([blocks[2].T, blocks[1]], axis=1)
         result = gram_iteration(jnp.concatenate([top, bottom], axis=0), scale, gram_scr, root_scr)
-        root[...] = result.astype(bf16)
+        result = result.astype(bf16)
+        root[:rows] = result[:rows, :rows]
+        root[rows:packed] = result[: rows // 2, rows:]
+        root[packed : packed + rows] = result[rows:, rows:]
+        root[packed + rows :] = result[rows // 2 : rows, rows:]
         for c in roots:
             c.start()
-        qall_ref[block, member, mine] = root[mine]
+        qall_ref[block, member, mine_q] = root[mine_q]
 
     walls = {}
 
@@ -656,13 +696,13 @@
     for d in (1, 3):
         plane_gather_turn(z, at_w(d), os_.at[d - 1], or_.at[d - 1], walls[d])
     for i, (here, _, _) in enumerate(parts):
-        arrival = remote(root.at[mine], qall_ref.at[block, i, mine], rs, rr.at[i], (to_core, z))
+        arrival = remote(root.at[mine_q], qall_ref.at[block, i, mine_q], rs, rr.at[i], (to_core, z))
 
         @pl.when(jnp.logical_not(here))
         def _():
             arrival.wait_recv()
 
-    at_q = block_at(qall_ref, 2, rows)
+    at_q = block_at(qall_ref, 2, packed)
     gathers_q = plane_gather_start(z, at_q, hs, hr)
     sends[2].wait_recv()
     walls[2] = plane_gather_start(z, at_w(2), os_.at[1], or_.at[1])
@@ -674,7 +714,7 @@
     plane_gather_finish(z, at_w(2), os_.at[1], or_.at[1], walls[2])
     most = pl.ds(0, 2 * rows - rows // 4)
     drain(gall.at[:, :, most], gs)
-    drain(qall_ref.at[:, :, most], hs)
+    drain(qall_ref.at[:, :, pl.ds(0, 2 * packed - packed // 4)], hs)
     for d in range(n_shard - 1):
         drain(wall_ref.at[d, :, most], os_.at[d])
     drain(held, ws)
@@ -682,7 +722,7 @@
 
     @pl.when(is_home)
     def _():
-        drain(u_ref.at[pl.ds(0, len(roots)), pl.ds(0, rows // 2)], rs)
+        drain(u_ref.at[pl.ds(0, len(roots)), pl.ds(0, packed * rows // cols)], rs)
 
     for here, part, cross in parts:
 
@@ -699,12 +739,13 @@
 
 def finish_kernel(
     owner_ref, mout_ref, u_ref, wall_ref, qall_ref, mom_out, update_out, owned_out,
-    ubuf, wbuf, msem, usem, wsem,
+    ubuf, wbuf, qbuf, msem, usem, wsem,
 ):
     f32 = jnp.float32
     slots, _, width = wbuf.shape
     mats, _, cols = ubuf.shape
     n_shard = width // cols
+    rows = qall_ref.shape[-1]
     z = lax.axis_index("shard")
     whole = pltpu.make_async_copy(mout_ref, mom_out, msem)
     whole.start()
@@ -714,7 +755,13 @@
 
     def update_one(m, carry):
         home, member = lodging(m)
-        ubuf[m] = jnp.dot(qall_ref[home, member], u_ref[m], preferred_element_type=f32)
+        q = qall_ref[home, member]
+        cross = jnp.concatenate([q[rows : 3 * rows // 2], q[5 * rows // 2 :]], axis=0)
+        qbuf[m, :rows, :rows] = q[:rows]
+        qbuf[m, :rows, rows:] = cross
+        qbuf[m, rows:, :rows] = cross.T
+        qbuf[m, rows:, rows:] = q[3 * rows // 2 : 5 * rows // 2]
+        ubuf[m] = jnp.dot(qbuf[m], u_ref[m], preferred_element_type=f32)
         put(ubuf, update_out, usem, m).start()
         return carry
 
@@ -728,8 +775,7 @@
             matrix = jnp.where(yes & (count == s), m, matrix)
             count = count + yes.astype(jnp.int32)
         keep = (count > s).astype(f32)
-        home, member = lodging(matrix)
-        q = qall_ref[home, member]
+        q = qbuf[matrix]
         for d in range(n_shard):
             right = u_ref[matrix] if d == 0 else wall_ref[d - 1, s]
             value = jnp.dot(q, right, preferred_element_type=f32) * keep
@@ -779,7 +825,7 @@
             pltpu.VMEM((MATS, KV, cols), f32),
             pltpu.VMEM((MATS, KV, cols), bf16),
             pltpu.VMEM((n_shard - 1, slots, KV, cols), bf16),
-            pltpu.VMEM((groups, members, KV, KV), bf16),
+            pltpu.VMEM((groups, members, 3 * rows, rows), bf16),
         ),
         in_specs=[SMEM_SPEC, SMEM_SPEC, ANY_SPEC, ANY_SPEC, ANY_SPEC],
         out_specs=(VMEM_SPEC,) * 4,
@@ -795,18 +841,17 @@
             pltpu.VMEM((n_shard, 3, rows, rows), f32),
             pltpu.VMEM((KV, KV), f32),
             pltpu.VMEM((KV, KV), f32),
-            pltpu.VMEM((KV, KV), bf16),
+            pltpu.VMEM((3 * rows, rows), bf16),
             [pltpu.VMEM((n_shard, n, tokens, cols), bf16) for n in shares],
             [pltpu.VMEM((n, tokens, 2 * KV), bf16) for n in shares],
             [pltpu.VMEM((n, 2, rows, tokens), bf16) for n in shares],
             [pltpu.VMEM((n_shard, 2, n, rows, cols), bf16) for n in shares],
             [pltpu.VMEM((n_shard, n, rows, cols), bf16) for n in shares],
             pltpu.VMEM((n_shard, members, rows, cols), bf16),
-            pltpu.VMEM((members, rows, cols), bf16),
-            pltpu.VMEM((n_shard - 1, members, rows, cols), bf16),
+            pltpu.VMEM((n_shard + 1, members, rows, cols), bf16),
             [dma((3 * n_shard + 3,)) for _ in range(2)]
             + [dma((4,)) for _ in range(3)]
-            + [dma((2,)), dma((2, n_shard)), dma((2,)), dma((n_shard - 1, 2))],
+            + [dma((2,)), dma((2, n_shard)), dma((2,)), dma((n_shard + 1, 2))],
             dma(()),
             dma(()), dma(()),
             dma(()), dma((10,)),
@@ -832,6 +877,7 @@
         scratch_shapes=[
             pltpu.VMEM(momentum.shape, f32),
             pltpu.VMEM((slots, KV, width), bf16),
+            pltpu.VMEM((MATS, KV, KV), bf16),
             dma(()), dma((MATS,)), dma((slots,)),
         ],
         compiler_params=params(20),

time: 113 us -> 105 us (0.929)
  Pallas kernels: 112 us -> 105 us
    pallas_call x1, Pallas kernels: 105 us -> 98 us  [per_device_planes(): pl.pallas_call(functools.partial(muon_kernel, n_shard, 1.0 / math.sqrt(to...]
where the time goes in v4:
time: 105 us
  Pallas kernels  105 us (100%)
    pallas_call x1, Pallas kernels, per_device_planes(): pl.pallas_call(functools.partial(muon_kernel, n_shard, 1.0 / math.sqrt(to...  98 us
    pallas_call x1, Pallas kernels, per_device_planes(): pl.pallas_call(finish_kernel, out_shape=(jax.ShapeDtypeStruct(momentum.sh...  6.57 us

profile of v4, /device:TPU:0, one launch (start us, length us, event | category | flops | bytes accessed | tf_op | source)
XLA Modules:
  0.0 105.3 jit_solution(4151934400197999153)
XLA Ops:
  0.6 0.0 copy-start
  0.6 98.0 %muon.1 = (f32[12,256,512]{2,1,0:T(8,128)S(1)}, bf16[12,256,512]{2,1,0:T(8,128)(2,1)S(1)}, bf16[3,4,256,512]{3,2,1,0:T(8,128)(2,1)S(1)}, bf16[4,3,384,128]{3,2,1,0:T(8,128)(2,1)S(1)}) custom-call(s32[12]{0:T(128)} %owner_ref.3, s32[2]{0:T(128)} %start_ref.1, bf16[6,128,2048]{2,1,0:T(8,128)(2,1)} %act_ref.1, bf16[6,128,512]{2,1,0:T(8,128)(2,1)} %cot_ref.1, ...), custom_call_target="tpu_custom_call" | custom-call | tf_op jit(solution)/shard_map/muon/pallas_call | solution.py:822
  98.7 0.0 copy-done
  98.7 6.6 %finish.1 = (f32[12,256,512]{2,1,0:T(8,128)}, f32[12,256,512]{2,1,0:T(8,128)}, bf16[4,256,2048]{2,1,0:T(8,128)(2,1)}) custom-call(s32[12]{0:T(128)S(1)} %copy-done, f32[12,256,512]{2,1,0:T(8,128)S(1)} %get-tuple-element.7.mout_ref, bf16[12,256,512]{2,1,0:T(8,128)(2,1)S(1)} %get-tuple-element.8.u_ref, bf16[3,4,256,512]{3,2,1,0:T(8,128)(2,1)S(1)} %get-tuple-element.9.wall_ref, ...), custom_call_target="tpu_custom_call" | custom-call | tf_op jit(solution)/shard_map/finish/pallas_call | solution.py:868
Async XLA Ops:
  0.6 98.1 %copy-start = (s32[12]{0:T(128)S(1)}, s32[12]{0:T(128)}, u32[]{:S(2)}) copy-start(s32[12]{0:T(128)} %owner_ref.3) | copy-start | bytes 148

commit v5 on v4

--- a/solution.py
+++ b/solution.py
@@ -146,10 +146,11 @@
     return me, core, x, y, to_core, to_x, to_y, to_xy
 
 
-def greet(peers):
+def greet(peers, meanwhile):
     barrier = pltpu.get_barrier_semaphore()
     for peer in peers:
         pl.semaphore_signal(barrier, inc=1, device_id=peer, device_id_type=MESH)
+    meanwhile()
     pl.semaphore_wait(barrier, len(peers))
 
 
@@ -289,15 +290,9 @@
         for key in keys:
             own[key].start()
 
-    def send(kind, k):
-        for j in range(counts[kind]):
-            hop[kind, k, j].start()
-
     def begin():
-        for key in keys[:6]:
+        for key in keys[:9]:
             hop[key].start()
-        send(1, 1)
-        send(0, 1)
         for key in keys:
             swap[key].start()
 
@@ -362,49 +357,51 @@
         take(0, 0, 0)
         turn(0, 0)
         product(1, 0)
+        hop[0, 2, 0].start()
         product(0, 0, 0)
-        send(1, 2)
+        hop[1, 2, 0].start()
         take(1, 1)
         take(0, n_shard, 1)
         product(1, 1)
-        send(0, 2)
+        hop[0, 2, 1].start()
+        hop[0, 3, 0].start()
         turn(0, 1)
         take(0, 0, 1)
         product(0, 0, 1)
         take(0, 1, 0)
         product(0, 1, 0)
-        send(1, 3)
+        hop[1, 3, 0].start()
         gather(0, 0)
         release(0, 0)
         take(0, 1, 1)
         product(0, 1, 1)
         take(1, 2)
         product(1, 2)
-        send(0, 3)
+        hop[0, 3, 1].start()
         gather(1, 0)
         release(1, 0)
+        take(0, 2, 0)
+        product(0, 2, 0)
         gather(0, 1)
         release(0, 1)
+        forward(0, 0)
         gather(1, 1)
         release(1, 1)
-        forward(0, 0)
-        take(0, 2, 0)
-        product(0, 2, 0)
         forward(1, 0)
         take(1, 3)
         product(1, 3)
         take(0, 2, 1)
         product(0, 2, 1)
+        take(0, 3, 0)
+        product(0, 3, 0)
+        gather(0, 2)
+        release(0, 2)
         forward(0, 1)
+        forward(0, 2)
         gather(1, 2)
         release(1, 2)
-        gather(0, 2)
-        release(0, 2)
         forward(1, 1)
-        forward(0, 2)
         forward(1, 2)
-        take(0, 3, 0)
-        product(0, 3, 0)
         take(0, 3, 1)
         product(0, 3, 1)
         gather(1, 3)
@@ -519,12 +516,11 @@
         n_shard, inverse, act_ref, cot_ref, gall, sqall, act, cot, turned, part, recv,
         plane, zrecv, *reduce_sems,
     )
-    enter()
     everyone = n_shard * 2 * gall.shape[0]
     here = me * n_shard + z
     others = [lax.rem(here + t, everyone) for t in range(1, everyone)]
     others = [(lax.div(to, n_shard), lax.rem(to, n_shard)) for to in others]
-    greet(others)
+    greet(others, enter)
 
     begin()
     fetch.start()
@@ -618,20 +614,21 @@
             count = count + yes.astype(jnp.int32)
         return found
 
+    partners = {
+        1: z + 1 - 2 * lax.rem(z, 2),
+        2: z + 2 - 4 * lax.div(z, 2),
+        3: n_shard - 1 - z,
+    }
     sends = {}
-
-    def send_slice(d):
-        shard = lax.rem(z + d, n_shard)
-        matrix = slot_matrix(shard, block)
+    walls = {}
+    for e in (1, 3, 2):
+        matrix = slot_matrix(partners[e], block)
         home, member = lodging(matrix)
-        held[d - 1] = advance(matrix, gall[home, member, mine], momentum[matrix, mine])[1]
-        sends[d] = remote(
-            held.at[d - 1], wall_ref.at[n_shard - d - 1, block, mine], ws, wr.at[d - 1], (me, shard)
+        held[e - 1] = advance(matrix, gall[home, member, mine], momentum[matrix, mine])[1]
+        sends[e] = remote(
+            held.at[e - 1], wall_ref.at[e - 1, block, mine], ws, wr.at[e - 1], (me, partners[e])
         )
-        sends[d].start()
-
-    send_slice(1)
-    send_slice(3)
+        sends[e].start()
 
     def all_one(m, carry):
         home, member = lodging(m)
@@ -639,6 +636,19 @@
         mout_ref[m] = new
         u_ref[m] = turned
         return carry
+
+    def wall_at(e):
+        return block_at(wall_ref.at[e - 1], 1, rows)
+
+    def wall_start(e):
+        sends[e].wait_recv()
+        walls[e] = plane_gather_start(z, wall_at(e), os_.at[e - 1], or_.at[e - 1])
+
+    def wall_turn(e):
+        plane_gather_turn(z, wall_at(e), os_.at[e - 1], or_.at[e - 1], walls[e])
+
+    def wall_finish(e):
+        plane_gather_finish(z, wall_at(e), os_.at[e - 1], or_.at[e - 1], walls[e])
 
     is_home = functools.reduce(jnp.logical_or, [here for here, _, _ in parts])
     member = jnp.where(z == HOMES[0][0], 0, 1 + core)
@@ -653,6 +663,12 @@
             half = 1 - core if d == 0 else c
             cut = pl.ds(pl.multiple_of(half * packed, packed), packed)
             roots.append(remote(root.at[cut], qall_ref.at[block, member, cut], rs, rr.at[member], peer))
+
+    @pl.when(jnp.logical_not(is_home))
+    def _():
+        lax.fori_loop(0, MATS, all_one, 0)
+
+    wall_start(1)
 
     @pl.when(is_home)
     def _():
@@ -683,18 +699,17 @@
             c.start()
         qall_ref[block, member, mine_q] = root[mine_q]
 
-    walls = {}
-
-    def at_w(d):
-        return block_at(wall_ref.at[n_shard - d - 1], 1, rows)
-
-    for d in (1, 3):
-        sends[d].wait_recv()
-        walls[d] = plane_gather_start(z, at_w(d), os_.at[d - 1], or_.at[d - 1])
-    send_slice(2)
-    lax.fori_loop(0, MATS, all_one, 0)
-    for d in (1, 3):
-        plane_gather_turn(z, at_w(d), os_.at[d - 1], or_.at[d - 1], walls[d])
+    wall_start(3)
+    wall_turn(1)
+
+    @pl.when(is_home)
+    def _():
+        lax.fori_loop(0, MATS, all_one, 0)
+
+    wall_start(2)
+    wall_turn(3)
+    wall_finish(1)
+    wall_turn(2)
     for i, (here, _, _) in enumerate(parts):
         arrival = remote(root.at[mine_q], qall_ref.at[block, i, mine_q], rs, rr.at[i], (to_core, z))
 
@@ -704,14 +719,10 @@
 
     at_q = block_at(qall_ref, 2, packed)
     gathers_q = plane_gather_start(z, at_q, hs, hr)
-    sends[2].wait_recv()
-    walls[2] = plane_gather_start(z, at_w(2), os_.at[1], or_.at[1])
-    for d in (1, 3):
-        plane_gather_finish(z, at_w(d), os_.at[d - 1], or_.at[d - 1], walls[d])
+    wall_finish(3)
+    wall_finish(2)
     plane_gather_turn(z, at_q, hs, hr, gathers_q)
-    plane_gather_turn(z, at_w(2), os_.at[1], or_.at[1], walls[2])
     plane_gather_finish(z, at_q, hs, hr, gathers_q)
-    plane_gather_finish(z, at_w(2), os_.at[1], or_.at[1], walls[2])
     most = pl.ds(0, 2 * rows - rows // 4)
     drain(gall.at[:, :, most], gs)
     drain(qall_ref.at[:, :, pl.ds(0, 2 * packed - packed // 4)], hs)
@@ -779,7 +790,7 @@
         for d in range(n_shard):
             right = u_ref[matrix] if d == 0 else wall_ref[d - 1, s]
             value = jnp.dot(q, right, preferred_element_type=f32) * keep
-            at = lax.rem(z + d, n_shard)
+            at = (z, z + 1 - 2 * lax.rem(z, 2), z + 2 - 4 * lax.div(z, 2), n_shard - 1 - z)[d]
             wbuf[s, :, pl.ds(pl.multiple_of(at * cols, cols), cols)] = value.astype(wbuf.dtype)
         put(wbuf, owned_out, wsem, s).start()
         return carry

time: 105 us -> 107 us (1.019)
    pallas_call x1, Pallas kernels: 98 us -> 99.8 us  [per_device_planes(): pl.pallas_call(functools.partial(muon_kernel, n_shard, 1.0 / math.sqrt(to...]
where the time goes in v5:
time: 107 us
  Pallas kernels  106 us (99%)
    pallas_call x1, Pallas kernels, per_device_planes(): pl.pallas_call(functools.partial(muon_kernel, n_shard, 1.0 / math.sqrt(to...  99.8 us
    pallas_call x1, Pallas kernels, per_device_planes(): pl.pallas_call(finish_kernel, out_shape=(jax.ShapeDtypeStruct(momentum.sh...  6.57 us

profile of v5, /device:TPU:0, one launch (start us, length us, event | category | flops | bytes accessed | tf_op | source)
XLA Modules:
  0.0 107.0 jit_solution(10775739682399822290)
XLA Ops:
  0.6 0.0 copy-start
  0.6 99.8 %muon.1 = (f32[12,256,512]{2,1,0:T(8,128)S(1)}, bf16[12,256,512]{2,1,0:T(8,128)(2,1)S(1)}, bf16[3,4,256,512]{3,2,1,0:T(8,128)(2,1)S(1)}, bf16[4,3,384,128]{3,2,1,0:T(8,128)(2,1)S(1)}) custom-call(s32[12]{0:T(128)} %owner_ref.3, s32[2]{0:T(128)} %start_ref.1, bf16[6,128,2048]{2,1,0:T(8,128)(2,1)} %act_ref.1, bf16[6,128,512]{2,1,0:T(8,128)(2,1)} %cot_ref.1, ...), custom_call_target="tpu_custom_call" | custom-call | tf_op jit(solution)/shard_map/muon/pallas_call | solution.py:833
  100.4 0.0 copy-done
  100.4 6.6 %finish.1 = (f32[12,256,512]{2,1,0:T(8,128)}, f32[12,256,512]{2,1,0:T(8,128)}, bf16[4,256,2048]{2,1,0:T(8,128)(2,1)}) custom-call(s32[12]{0:T(128)S(1)} %copy-done, f32[12,256,512]{2,1,0:T(8,128)S(1)} %get-tuple-element.7.mout_ref, bf16[12,256,512]{2,1,0:T(8,128)(2,1)S(1)} %get-tuple-element.8.u_ref, bf16[3,4,256,512]{3,2,1,0:T(8,128)(2,1)S(1)} %get-tuple-element.9.wall_ref, ...), custom_call_target="tpu_custom_call" | custom-call | tf_op jit(solution)/shard_map/finish/pallas_call | solution.py:879
Async XLA Ops:
  0.6 99.8 %copy-start = (s32[12]{0:T(128)S(1)}, s32[12]{0:T(128)}, u32[]{:S(2)}) copy-start(s32[12]{0:T(128)} %owner_ref.3) | copy-start | bytes 148

commit v6 on v5

--- a/solution.py
+++ b/solution.py
@@ -160,45 +160,43 @@
     )
 
 
-def plane_gather_start(z, at, send, recv):
-    me, core, x, y, to_core, to_x, to_y, to_xy = place()
-    plan = ((0, to_x, 0), (2, to_y, 1), (1, to_x, 1), (3, to_y, 0), (4, to_core, None))
-    copies = {}
-    for k, peer, half in plan:
-        copies[k] = remote(at(me, half), at(me, half), send, recv.at[k], (peer, z))
-        copies[k].start()
-    return copies
-
-
-def plane_gather_turn(z, at, send, recv, copies):
-    me, core, x, y, to_core, to_x, to_y, to_xy = place()
-
-    def forward(k, block, half, peer):
-        copies[k] = remote(
-            at(block, half), at(block, half), send, recv.at[k], (peer, z)
-        )
-        copies[k].start()
-
-    copies[0].wait_recv()
-    forward(5, to_x, 0, to_y)
-    copies[2].wait_recv()
-    forward(6, to_y, 1, to_x)
-    copies[1].wait_recv()
-    forward(7, to_x, None, to_core)
-    copies[3].wait_recv()
-    forward(8, to_y, None, to_core)
-
-
-def plane_gather_finish(z, at, send, recv, copies, last=(4, 7, 8, 9)):
-    me, core, x, y, to_core, to_x, to_y, to_xy = place()
-    copies[5].wait_recv()
-    copies[6].wait_recv()
-    copies[9] = remote(
-        at(to_xy, None), at(to_xy, None), send, recv.at[9], (to_core, z)
-    )
-    copies[9].start()
-    for k in last:
-        copies[k].wait_recv()
+class PlaneGather:
+    def __init__(self, z, at, send, recv):
+        self.z, self.at, self.send, self.recv = z, at, send, recv
+        self.copies = {}
+
+    def go(self, k, block, half, peer):
+        ref = self.at(block, half)
+        self.copies[k] = remote(ref, ref, self.send, self.recv.at[k], (peer, self.z))
+        self.copies[k].start()
+
+    def wait(self, *ks):
+        for k in ks:
+            self.copies[k].wait_recv()
+
+    def begin(self):
+        me, core, x, y, to_core, to_x, to_y, to_xy = place()
+        for k, peer, half in ((0, to_x, 0), (2, to_y, 1), (1, to_x, 1), (3, to_y, 0), (4, to_core, None)):
+            self.go(k, me, half, peer)
+
+    def turn(self):
+        me, core, x, y, to_core, to_x, to_y, to_xy = place()
+        self.wait(0)
+        self.go(5, to_x, 0, to_y)
+        self.wait(2)
+        self.go(6, to_y, 1, to_x)
+
+    def share(self):
+        me, core, x, y, to_core, to_x, to_y, to_xy = place()
+        self.wait(1)
+        self.go(7, to_x, None, to_core)
+        self.wait(3)
+        self.go(8, to_y, None, to_core)
+
+    def corner(self):
+        me, core, x, y, to_core, to_x, to_y, to_xy = place()
+        self.wait(5, 6)
+        self.go(9, to_xy, None, to_core)
 
 
 def drain(ref, semaphore):
@@ -529,7 +527,8 @@
     for peer in others:
         remote(sqall.at[here], sqall.at[here], ps, pr, peer).start()
     at_g = block_at(gall, 2, rows)
-    gathers = plane_gather_start(z, at_g, gs, gr)
+    gather_g = PlaneGather(z, at_g, gs, gr)
+    gather_g.begin()
     fetch.wait()
     drain(sqall.at[pl.ds(0, everyone - 1)], pr)
 
@@ -562,7 +561,8 @@
         new = momentum_rate * past + step
         return new, (step + momentum_rate * new).astype(bf16)
 
-    gathers[4].wait_recv()
+    gather_g.turn()
+    gather_g.wait(4)
     for i in range(members):
         layer, side = lodged(block, i)
         matrix = 2 * layer + side
@@ -602,8 +602,9 @@
             def _():
                 cross.start()
 
-    plane_gather_turn(z, at_g, gs, gr, gathers)
-    plane_gather_finish(z, at_g, gs, gr, gathers, last=(7, 8, 9))
+    gather_g.share()
+    gather_g.corner()
+    gather_g.wait(7, 8, 9)
 
     def slot_matrix(shard, slot):
         found = jnp.int32(0)
@@ -621,7 +622,8 @@
     }
     sends = {}
     walls = {}
-    for e in (1, 3, 2):
+
+    def send_slice(e):
         matrix = slot_matrix(partners[e], block)
         home, member = lodging(matrix)
         held[e - 1] = advance(matrix, gall[home, member, mine], momentum[matrix, mine])[1]
@@ -630,6 +632,9 @@
         )
         sends[e].start()
 
+    send_slice(1)
+    send_slice(3)
+
     def all_one(m, carry):
         home, member = lodging(m)
         new, turned = advance(m, gall[home, member], momentum[m])
@@ -637,18 +642,11 @@
         u_ref[m] = turned
         return carry
 
-    def wall_at(e):
-        return block_at(wall_ref.at[e - 1], 1, rows)
-
-    def wall_start(e):
+    def wall_begin(e):
         sends[e].wait_recv()
-        walls[e] = plane_gather_start(z, wall_at(e), os_.at[e - 1], or_.at[e - 1])
-
-    def wall_turn(e):
-        plane_gather_turn(z, wall_at(e), os_.at[e - 1], or_.at[e - 1], walls[e])
-
-    def wall_finish(e):
-        plane_gather_finish(z, wall_at(e), os_.at[e - 1], or_.at[e - 1], walls[e])
+        at = block_at(wall_ref.at[e - 1], 1, rows)
+        walls[e] = PlaneGather(z, at, os_.at[e - 1], or_.at[e - 1])
+        walls[e].begin()
 
     is_home = functools.reduce(jnp.logical_or, [here for here, _, _ in parts])
     member = jnp.where(z == HOMES[0][0], 0, 1 + core)
@@ -667,8 +665,6 @@
     @pl.when(jnp.logical_not(is_home))
     def _():
         lax.fori_loop(0, MATS, all_one, 0)
-
-    wall_start(1)
 
     @pl.when(is_home)
     def _():
@@ -699,30 +695,38 @@
             c.start()
         qall_ref[block, member, mine_q] = root[mine_q]
 
-    wall_start(3)
-    wall_turn(1)
+    wall_begin(1)
+    wall_begin(3)
+    send_slice(2)
+    walls[1].turn()
+    walls[1].share()
+    walls[3].turn()
+    walls[1].corner()
+    for i, (here, _, _) in enumerate(parts):
+        arrival = remote(root.at[mine_q], qall_ref.at[block, i, mine_q], rs, rr.at[i], (to_core, z))
+
+        @pl.when(jnp.logical_not(here))
+        def _():
+            arrival.wait_recv()
+
+    gather_q = PlaneGather(z, block_at(qall_ref, 2, packed), hs, hr)
+    gather_q.begin()
+    walls[3].share()
+    wall_begin(2)
+    walls[3].corner()
+    gather_q.turn()
+    gather_q.share()
+    walls[2].turn()
 
     @pl.when(is_home)
     def _():
         lax.fori_loop(0, MATS, all_one, 0)
 
-    wall_start(2)
-    wall_turn(3)
-    wall_finish(1)
-    wall_turn(2)
-    for i, (here, _, _) in enumerate(parts):
-        arrival = remote(root.at[mine_q], qall_ref.at[block, i, mine_q], rs, rr.at[i], (to_core, z))
-
-        @pl.when(jnp.logical_not(here))
-        def _():
-            arrival.wait_recv()
-
-    at_q = block_at(qall_ref, 2, packed)
-    gathers_q = plane_gather_start(z, at_q, hs, hr)
-    wall_finish(3)
-    wall_finish(2)
-    plane_gather_turn(z, at_q, hs, hr, gathers_q)
-    plane_gather_finish(z, at_q, hs, hr, gathers_q)
+    gather_q.corner()
+    walls[2].share()
+    walls[2].corner()
+    for gather in (walls[1], walls[3], gather_q, walls[2]):
+        gather.wait(4, 7, 8, 9)
     most = pl.ds(0, 2 * rows - rows // 4)
     drain(gall.at[:, :, most], gs)
     drain(qall_ref.at[:, :, pl.ds(0, 2 * packed - packed // 4)], hs)
@@ -776,7 +780,7 @@
         put(ubuf, update_out, usem, m).start()
         return carry
 
-    lax.fori_loop(0, mats, update_one, 0)
+    lax.fori_loop(0, mats, update_one, 0, unroll=3)
 
     def owned_one(s, carry):
         matrix = jnp.int32(0)
@@ -795,7 +799,7 @@
         put(wbuf, owned_out, wsem, s).start()
         return carry
 
-    lax.fori_loop(0, slots, owned_one, 0)
+    lax.fori_loop(0, slots, owned_one, 0, unroll=2)
 
     def each(count, buf, out, sem):
         def step(m, carry):

time: 107 us -> 108 us (level)
  no operation moved by 1% of the time
where the time goes in v6:
time: 108 us; the launch traced here: 107 us
  Pallas kernels  107 us (99%)
    pallas_call x1, Pallas kernels, per_device_planes(): pl.pallas_call(functools.partial(muon_kernel, n_shard, 1.0 / math.sqrt(to...  100 us
    pallas_call x1, Pallas kernels, per_device_planes(): pl.pallas_call(finish_kernel, out_shape=(jax.ShapeDtypeStruct(momentum.sh...  6.57 us

profile of v6, /device:TPU:0, one launch (start us, length us, event | category | flops | bytes accessed | tf_op | source)
XLA Modules:
  0.0 107.5 jit_solution(3905535895207276924)
XLA Ops:
  0.6 0.0 copy-start
  0.6 100.2 %muon.1 = (f32[12,256,512]{2,1,0:T(8,128)S(1)}, bf16[12,256,512]{2,1,0:T(8,128)(2,1)S(1)}, bf16[3,4,256,512]{3,2,1,0:T(8,128)(2,1)S(1)}, bf16[4,3,384,128]{3,2,1,0:T(8,128)(2,1)S(1)}) custom-call(s32[12]{0:T(128)} %owner_ref.3, s32[2]{0:T(128)} %start_ref.1, bf16[6,128,2048]{2,1,0:T(8,128)(2,1)} %act_ref.1, bf16[6,128,512]{2,1,0:T(8,128)(2,1)} %cot_ref.1, ...), custom_call_target="tpu_custom_call" | custom-call | tf_op jit(solution)/shard_map/muon/pallas_call | solution.py:837
  100.9 0.0 copy-done
  100.9 6.6 %finish.1 = (f32[12,256,512]{2,1,0:T(8,128)}, f32[12,256,512]{2,1,0:T(8,128)}, bf16[4,256,2048]{2,1,0:T(8,128)(2,1)}) custom-call(s32[12]{0:T(128)S(1)} %copy-done, f32[12,256,512]{2,1,0:T(8,128)S(1)} %get-tuple-element.7.mout_ref, bf16[12,256,512]{2,1,0:T(8,128)(2,1)S(1)} %get-tuple-element.8.u_ref, bf16[3,4,256,512]{3,2,1,0:T(8,128)(2,1)S(1)} %get-tuple-element.9.wall_ref, ...), custom_call_target="tpu_custom_call" | custom-call | tf_op jit(solution)/shard_map/finish/pallas_call | solution.py:883
Async XLA Ops:
  0.6 100.3 %copy-start = (s32[12]{0:T(128)S(1)}, s32[12]{0:T(128)}, u32[]{:S(2)}) copy-start(s32[12]{0:T(128)} %owner_ref.3) | copy-start | bytes 148

commit v7 on v4

--- a/solution.py
+++ b/solution.py
@@ -146,10 +146,11 @@
     return me, core, x, y, to_core, to_x, to_y, to_xy
 
 
-def greet(peers):
+def greet(peers, meanwhile):
     barrier = pltpu.get_barrier_semaphore()
     for peer in peers:
         pl.semaphore_signal(barrier, inc=1, device_id=peer, device_id_type=MESH)
+    meanwhile()
     pl.semaphore_wait(barrier, len(peers))
 
 
@@ -289,15 +290,9 @@
         for key in keys:
             own[key].start()
 
-    def send(kind, k):
-        for j in range(counts[kind]):
-            hop[kind, k, j].start()
-
     def begin():
-        for key in keys[:6]:
+        for key in keys[:9]:
             hop[key].start()
-        send(1, 1)
-        send(0, 1)
         for key in keys:
             swap[key].start()
 
@@ -362,49 +357,51 @@
         take(0, 0, 0)
         turn(0, 0)
         product(1, 0)
+        hop[0, 2, 0].start()
         product(0, 0, 0)
-        send(1, 2)
+        hop[1, 2, 0].start()
         take(1, 1)
         take(0, n_shard, 1)
         product(1, 1)
-        send(0, 2)
+        hop[0, 2, 1].start()
+        hop[0, 3, 0].start()
         turn(0, 1)
         take(0, 0, 1)
         product(0, 0, 1)
         take(0, 1, 0)
         product(0, 1, 0)
-        send(1, 3)
+        hop[1, 3, 0].start()
         gather(0, 0)
         release(0, 0)
         take(0, 1, 1)
         product(0, 1, 1)
         take(1, 2)
         product(1, 2)
-        send(0, 3)
+        hop[0, 3, 1].start()
         gather(1, 0)
         release(1, 0)
+        take(0, 2, 0)
+        product(0, 2, 0)
         gather(0, 1)
         release(0, 1)
+        forward(0, 0)
         gather(1, 1)
         release(1, 1)
-        forward(0, 0)
-        take(0, 2, 0)
-        product(0, 2, 0)
         forward(1, 0)
         take(1, 3)
         product(1, 3)
         take(0, 2, 1)
         product(0, 2, 1)
+        take(0, 3, 0)
+        product(0, 3, 0)
+        gather(0, 2)
+        release(0, 2)
         forward(0, 1)
+        forward(0, 2)
         gather(1, 2)
         release(1, 2)
-        gather(0, 2)
-        release(0, 2)
         forward(1, 1)
-        forward(0, 2)
         forward(1, 2)
-        take(0, 3, 0)
-        product(0, 3, 0)
         take(0, 3, 1)
         product(0, 3, 1)
         gather(1, 3)
@@ -451,7 +448,7 @@
     return enter, begin, run, leave
 
 
-HOMES = ((1, 0), (2, 0), (2, 1))
+HOMES = ((2, 0), (1, 0), (1, 1))
 
 
 def block_at(ref, axis, rows):
@@ -519,12 +516,11 @@
         n_shard, inverse, act_ref, cot_ref, gall, sqall, act, cot, turned, part, recv,
         plane, zrecv, *reduce_sems,
     )
-    enter()
     everyone = n_shard * 2 * gall.shape[0]
     here = me * n_shard + z
     others = [lax.rem(here + t, everyone) for t in range(1, everyone)]
     others = [(lax.div(to, n_shard), lax.rem(to, n_shard)) for to in others]
-    greet(others)
+    greet(others, enter)
 
     begin()
     fetch.start()
@@ -747,11 +743,12 @@
     n_shard = width // cols
     rows = qall_ref.shape[-1]
     z = lax.axis_index("shard")
-    whole = pltpu.make_async_copy(mout_ref, mom_out, msem)
-    whole.start()
 
     def put(buf, out, sem, m):
-        return pltpu.make_async_copy(buf.at[m], out.at[m], sem.at[m])
+        return pltpu.make_async_copy(buf.at[m], out.at[m], sem)
+
+    for m in range(mats):
+        put(mout_ref, mom_out, msem, m).start()
 
     def update_one(m, carry):
         home, member = lodging(m)
@@ -765,7 +762,7 @@
         put(ubuf, update_out, usem, m).start()
         return carry
 
-    lax.fori_loop(0, mats, update_one, 0)
+    lax.fori_loop(0, mats, update_one, 0, unroll=3)
 
     def owned_one(s, carry):
         matrix = jnp.int32(0)
@@ -784,18 +781,11 @@
         put(wbuf, owned_out, wsem, s).start()
         return carry
 
-    lax.fori_loop(0, slots, owned_one, 0)
-
-    def each(count, buf, out, sem):
-        def step(m, carry):
-            put(buf, out, sem, m).wait()
-            return carry
-
-        lax.fori_loop(0, count, step, 0)
-
-    whole.wait()
-    each(mats, ubuf, update_out, usem)
-    each(slots, wbuf, owned_out, wsem)
+    lax.fori_loop(0, slots, owned_one, 0, unroll=2)
+
+    drain(mout_ref, msem)
+    drain(ubuf, usem)
+    drain(wbuf, wsem)
 
 
 def per_device_planes(activations, cotangents, momentum, owners, bucket_starts):
@@ -878,7 +868,7 @@
             pltpu.VMEM(momentum.shape, f32),
             pltpu.VMEM((slots, KV, width), bf16),
             pltpu.VMEM((MATS, KV, KV), bf16),
-            dma(()), dma((MATS,)), dma((slots,)),
+            dma(()), dma(()), dma(()),
         ],
         compiler_params=params(20),
         name="finish",

time: 105 us -> 104 us (level)
  Pallas kernels: 105 us -> 103 us
    pallas_call x1, Pallas kernels: 98 us -> 96.9 us  [per_device_planes(): pl.pallas_call(functools.partial(muon_kernel, n_shard, 1.0 / math.sqrt(to...]
where the time goes in v7:
time: 104 us
  Pallas kernels  103 us (99%)
    pallas_call x1, Pallas kernels, per_device_planes(): pl.pallas_call(functools.partial(muon_kernel, n_shard, 1.0 / math.sqrt(to...  96.9 us
    pallas_call x1, Pallas kernels, per_device_planes(): pl.pallas_call(finish_kernel, out_shape=(jax.ShapeDtypeStruct(momentum.sh...  6.38 us

profile of v7, /device:TPU:0, one launch (start us, length us, event | category | flops | bytes accessed | tf_op | source)
XLA Modules:
  0.0 104.0 jit_solution(11170213625949053889)
XLA Ops:
  0.6 0.0 copy-start
  0.6 96.9 %muon.1 = (f32[12,256,512]{2,1,0:T(8,128)S(1)}, bf16[12,256,512]{2,1,0:T(8,128)(2,1)S(1)}, bf16[3,4,256,512]{3,2,1,0:T(8,128)(2,1)S(1)}, bf16[4,3,384,128]{3,2,1,0:T(8,128)(2,1)S(1)}) custom-call(s32[12]{0:T(128)} %owner_ref.3, s32[2]{0:T(128)} %start_ref.1, bf16[6,128,2048]{2,1,0:T(8,128)(2,1)} %act_ref.1, bf16[6,128,512]{2,1,0:T(8,128)(2,1)} %cot_ref.1, ...), custom_call_target="tpu_custom_call" | custom-call | tf_op jit(solution)/shard_map/muon/pallas_call | solution.py:812
  97.6 0.0 copy-done
  97.6 6.4 %finish.1 = (f32[12,256,512]{2,1,0:T(8,128)}, f32[12,256,512]{2,1,0:T(8,128)}, bf16[4,256,2048]{2,1,0:T(8,128)(2,1)}) custom-call(s32[12]{0:T(128)S(1)} %copy-done, f32[12,256,512]{2,1,0:T(8,128)S(1)} %get-tuple-element.7.mout_ref, bf16[12,256,512]{2,1,0:T(8,128)(2,1)S(1)} %get-tuple-element.8.u_ref, bf16[3,4,256,512]{3,2,1,0:T(8,128)(2,1)S(1)} %get-tuple-element.9.wall_ref, ...), custom_call_target="tpu_custom_call" | custom-call | tf_op jit(solution)/shard_map/finish/pallas_call | solution.py:858
Async XLA Ops:
  0.6 96.9 %copy-start = (s32[12]{0:T(128)S(1)}, s32[12]{0:T(128)}, u32[]{:S(2)}) copy-start(s32[12]{0:T(128)} %owner_ref.3) | copy-start | bytes 148

commit v8 on v7

--- a/solution.py
+++ b/solution.py
@@ -616,7 +616,7 @@
 
     sends = {}
 
-    def send_slice(d):
+    def make_slice(d):
         shard = lax.rem(z + d, n_shard)
         matrix = slot_matrix(shard, block)
         home, member = lodging(matrix)
@@ -624,10 +624,16 @@
         sends[d] = remote(
             held.at[d - 1], wall_ref.at[n_shard - d - 1, block, mine], ws, wr.at[d - 1], (me, shard)
         )
+
+    for d in (1, 3):
+        make_slice(d)
         sends[d].start()
-
-    send_slice(1)
-    send_slice(3)
+    make_slice(2)
+    early = z == 2
+
+    @pl.when(early)
+    def _():
+        sends[2].start()
 
     def all_one(m, carry):
         home, member = lodging(m)
@@ -649,6 +655,10 @@
             half = 1 - core if d == 0 else c
             cut = pl.ds(pl.multiple_of(half * packed, packed), packed)
             roots.append(remote(root.at[cut], qall_ref.at[block, member, cut], rs, rr.at[member], peer))
+
+    @pl.when(jnp.logical_not(is_home))
+    def _():
+        lax.fori_loop(0, MATS, all_one, 0)
 
     @pl.when(is_home)
     def _():
@@ -687,8 +697,15 @@
     for d in (1, 3):
         sends[d].wait_recv()
         walls[d] = plane_gather_start(z, at_w(d), os_.at[d - 1], or_.at[d - 1])
-    send_slice(2)
-    lax.fori_loop(0, MATS, all_one, 0)
+
+    @pl.when(jnp.logical_not(early))
+    def _():
+        sends[2].start()
+
+    @pl.when(is_home)
+    def _():
+        lax.fori_loop(0, MATS, all_one, 0)
+
     for d in (1, 3):
         plane_gather_turn(z, at_w(d), os_.at[d - 1], or_.at[d - 1], walls[d])
     for i, (here, _, _) in enumerate(parts):

time: 104 us -> 104 us (level)
  no operation moved by 1% of the time
where the time goes in v8:
time: 104 us
  Pallas kernels  103 us (99%)
    pallas_call x1, Pallas kernels, per_device_planes(): pl.pallas_call(functools.partial(muon_kernel, n_shard, 1.0 / math.sqrt(to...  97 us
    pallas_call x1, Pallas kernels, per_device_planes(): pl.pallas_call(finish_kernel, out_shape=(jax.ShapeDtypeStruct(momentum.sh...  6.38 us

profile of v8, /device:TPU:0, one launch (start us, length us, event | category | flops | bytes accessed | tf_op | source)
XLA Modules:
  0.0 104.0 jit_solution(2136658837632789778)
XLA Ops:
  0.6 0.0 copy-start
  0.6 97.0 %muon.1 = (f32[12,256,512]{2,1,0:T(8,128)S(1)}, bf16[12,256,512]{2,1,0:T(8,128)(2,1)S(1)}, bf16[3,4,256,512]{3,2,1,0:T(8,128)(2,1)S(1)}, bf16[4,3,384,128]{3,2,1,0:T(8,128)(2,1)S(1)}) custom-call(s32[12]{0:T(128)} %owner_ref.3, s32[2]{0:T(128)} %start_ref.1, bf16[6,128,2048]{2,1,0:T(8,128)(2,1)} %act_ref.1, bf16[6,128,512]{2,1,0:T(8,128)(2,1)} %cot_ref.1, ...), custom_call_target="tpu_custom_call" | custom-call | tf_op jit(solution)/shard_map/muon/pallas_call | solution.py:829
  97.6 0.0 copy-done
  97.6 6.4 %finish.1 = (f32[12,256,512]{2,1,0:T(8,128)}, f32[12,256,512]{2,1,0:T(8,128)}, bf16[4,256,2048]{2,1,0:T(8,128)(2,1)}) custom-call(s32[12]{0:T(128)S(1)} %copy-done, f32[12,256,512]{2,1,0:T(8,128)S(1)} %get-tuple-element.7.mout_ref, bf16[12,256,512]{2,1,0:T(8,128)(2,1)S(1)} %get-tuple-element.8.u_ref, bf16[3,4,256,512]{3,2,1,0:T(8,128)(2,1)S(1)} %get-tuple-element.9.wall_ref, ...), custom_call_target="tpu_custom_call" | custom-call | tf_op jit(solution)/shard_map/finish/pallas_call | solution.py:875
Async XLA Ops:
  0.6 97.0 %copy-start = (s32[12]{0:T(128)S(1)}, s32[12]{0:T(128)}, u32[]{:S(2)}) copy-start(s32[12]{0:T(128)} %owner_ref.3) | copy-start | bytes 148
